TPU v7x, 32 devices: a whole 2x2x4 slice. The times are simulated.
32 devices in a mesh: ctx: 8 (over z, x), exp: 4 (over y, core).
Axes of the slice: x: 2, y: 2, z: 4, core: 2. Of those that a mesh axis runs over, the one named last changes fastest.
Arguments:
- tokens: bfloat16 [2, 4, 1024, 1024], P(None, 'exp', 'ctx'), may hold values from -6 to 6
- cotangent: bfloat16 [2, 4, 1024, 1024], P(None, 'exp', 'ctx'), may hold values from -6 to 6
- bucket_ids: int32 [2048], replicated, may hold values from 0 to 31
- routes: int32 [2, 4, 1024, 2], P(None, 'exp', 'ctx'), may hold values from 0 to 3, all different within a row; in each aligned block of 128 rows (0 to 127, 128 to 255, ..., all dimensions but the last counted through in order) at most 80 rows name the same one
- qkv_master: float32 [3, 1024, 1024], P(None, ('ctx', 'exp')), may hold values from -0.1875 to 0.1875
- out_master: float32 [1024, 1024], P(('ctx', 'exp')), may hold values from -1.5 to 1.5
- router_master: float32 [1024, 4], P(('ctx', 'exp')), may hold values from -0.375 to 0.375
- gain_attn_master: float32 [1024], P(('ctx', 'exp')), may hold values from 0.5 to 1.5
- gain_mix_master: float32 [1024], P(('ctx', 'exp')), may hold values from 0.5 to 1.5
- table_master: float32 [512], P(('ctx', 'exp')), may hold values from -4 to 4
- gate_master: float32 [4, 1024, 2816], P('exp', 'ctx'), may hold values from -0.1875 to 0.1875
- up_master: float32 [4, 1024, 2816], P('exp', 'ctx'), may hold values from -0.1875 to 0.1875
- down_master: float32 [4, 2816, 1024], P('exp', 'ctx'), may hold values from -0.109375 to 0.109375
- qkv_first: float32 [3, 1024, 1024], P(None, ('ctx', 'exp')), may hold values from -543.058 to 543.058
- out_first: float32 [1024, 1024], P(('ctx', 'exp')), may hold values from -13.57645 to 13.57645
- router_first: float32 [1024, 4], P(('ctx', 'exp')), may hold values from -814.58701 to 814.58701
- gain_attn_first: float32 [1024], P(('ctx', 'exp')), may hold values from -2715.29 to 2715.29
- gain_mix_first: float32 [1024], P(('ctx', 'exp')), may hold values from -271.529 to 271.529
- table_first: float32 [512], P(('ctx', 'exp')), may hold values from -814.58701 to 814.58701
- gate_first: float32 [4, 1024, 2816], P('exp', 'ctx'), may hold values from -27.1529 to 27.1529
- up_first: float32 [4, 1024, 2816], P('exp', 'ctx'), may hold values from -27.1529 to 27.1529
- down_first: float32 [4, 2816, 1024], P('exp', 'ctx'), may hold values from -54.3058 to 54.3058
- qkv_second: float32 [3, 1024, 1024], P(None, ('ctx', 'exp')), may hold values from 9830.4 to 98304
- out_second: float32 [1024, 1024], P(('ctx', 'exp')), may hold values from 6.144 to 61.44
- router_second: float32 [1024, 4], P(('ctx', 'exp')), may hold values from 22118.4 to 221184
- gain_attn_second: float32 [1024], P(('ctx', 'exp')), may hold values from 245760 to 2457600
- gain_mix_second: float32 [1024], P(('ctx', 'exp')), may hold values from 2457.6 to 24576
- table_second: float32 [512], P(('ctx', 'exp')), may hold values from 22118.4 to 221184
- gate_second: float32 [4, 1024, 2816], P('exp', 'ctx'), may hold values from 24.576 to 245.76
- up_second: float32 [4, 1024, 2816], P('exp', 'ctx'), may hold values from 24.576 to 245.76
- down_second: float32 [4, 2816, 1024], P('exp', 'ctx'), may hold values from 98.304 to 983.04
Outputs:
- output: bfloat16 [2, 4, 1024, 1024], P(None, 'exp', 'ctx')
- grad_tokens: float32 [2, 4, 1024, 1024], P(None, 'exp', 'ctx')
- qkv_grad: float32 [3, 1024, 1024], P(None, ('ctx', 'exp'))
- out_grad: float32 [1024, 1024], P(('ctx', 'exp'))
- router_grad: float32 [1024, 4], P(('ctx', 'exp'))
- gain_attn_grad: float32 [1024], P(('ctx', 'exp'))
- gain_mix_grad: float32 [1024], P(('ctx', 'exp'))
- table_grad: float32 [512], P(('ctx', 'exp'))
- gate_grad: float32 [4, 1024, 2816], P('exp', 'ctx')
- up_grad: float32 [4, 1024, 2816], P('exp', 'ctx')
- down_grad: float32 [4, 2816, 1024], P('exp', 'ctx')
- qkv_first_new: float32 [3, 1024, 1024], P(None, ('ctx', 'exp'))
- out_first_new: float32 [1024, 1024], P(('ctx', 'exp'))
- router_first_new: float32 [1024, 4], P(('ctx', 'exp'))
- gain_attn_first_new: float32 [1024], P(('ctx', 'exp'))
- gain_mix_first_new: float32 [1024], P(('ctx', 'exp'))
- table_first_new: float32 [512], P(('ctx', 'exp'))
- gate_first_new: float32 [4, 1024, 2816], P('exp', 'ctx')
- up_first_new: float32 [4, 1024, 2816], P('exp', 'ctx')
- down_first_new: float32 [4, 2816, 1024], P('exp', 'ctx')
- qkv_second_new: float32 [3, 1024, 1024], P(None, ('ctx', 'exp'))
- out_second_new: float32 [1024, 1024], P(('ctx', 'exp'))
- router_second_new: float32 [1024, 4], P(('ctx', 'exp'))
- gain_attn_second_new: float32 [1024], P(('ctx', 'exp'))
- gain_mix_second_new: float32 [1024], P(('ctx', 'exp'))
- table_second_new: float32 [512], P(('ctx', 'exp'))
- gate_second_new: float32 [4, 1024, 2816], P('exp', 'ctx')
- up_second_new: float32 [4, 1024, 2816], P('exp', 'ctx')
- down_second_new: float32 [4, 2816, 1024], P('exp', 'ctx')
- qkv_update: float32 [3, 1024, 1024], P(None, ('ctx', 'exp'))
- out_update: float32 [1024, 1024], P(('ctx', 'exp'))
- router_update: float32 [1024, 4], P(('ctx', 'exp'))
- gain_attn_update: float32 [1024], P(('ctx', 'exp'))
- gain_mix_update: float32 [1024], P(('ctx', 'exp'))
- table_update: float32 [512], P(('ctx', 'exp'))
- gate_update: float32 [4, 1024, 2816], P('exp', 'ctx')
- up_update: float32 [4, 1024, 2816], P('exp', 'ctx')
- down_update: float32 [4, 2816, 1024], P('exp', 'ctx')
Inputs may be any that keep to these rules, and one draw needn't show every extreme that they name: `routes`: in each aligned block of 128 tokens (one index of ctx, one sequence) no expert is named by more than 80 choices, and in some block one expert is named exactly 80 times; the two experts of a token differ.
All inputs are finite; a program needn't handle non-finite values.
Results may differ from a plain program's by a relative error of at most 0.024.
The roundings to bfloat16 on the way count: a program that leaves them out, or rounds other values in their place, can miss the bound.
Values may be sent and summed in bfloat16 or wider, within the bound.
A program may use at most 256 MiB of HBM per device.

v0:
```python
from functools import partial
import math

import jax
import jax.numpy as jnp
from jax import lax
from jax.sharding import PartitionSpec as P

D = 1024
HEADS = 16
HEAD_DIM = 64
TOP = 2
BLOCK = 256
STEP = 3


eps_norm = 1e-06
eps_adam = 1e-08
score_scale = 0.125
decay_rate = 0.5
learn_rate = 1.0
weight_decay = 0.1
highest = lax.Precision.HIGHEST
last_dims = (((1,), (1,)), ((), ()))
first_dims = (((0,), (0,)), ((), ()))


def passed_along(value, axis, steps):
    count = lax.axis_size(axis)
    pairs = [(source, (source + steps) % count) for source in range(count)]
    return lax.ppermute(value, axis, pairs)


def window_start(first_query, first_key, query_count, offset_bias):
    length = offset_bias.shape[1] // 2
    return first_key - first_query + length - query_count


def skew_bias(offset_bias, first_query, first_key, query_count, key_count):
    width = query_count + key_count - 1
    start = window_start(first_query, first_key, query_count, offset_bias)
    window = lax.dynamic_slice_in_dim(offset_bias, start, width, 1)
    head_count = window.shape[0]
    tiled = jnp.broadcast_to(window[:, None, :], (head_count, query_count, width))
    padded = jnp.pad(tiled, ((0, 0), (0, 0), (0, 1)))
    flat = padded.reshape(head_count, query_count * (width + 1))[:, : query_count * width]
    skewed = flat.reshape(head_count, query_count, width)
    return skewed[:, :, query_count - 1 :]


def diagonal_sums(grad_block, query_count, key_count):
    head_count = grad_block.shape[0]
    width = query_count + key_count - 1
    flipped = grad_block[:, ::-1, :]
    padded = jnp.pad(flipped, ((0, 0), (0, 0), (0, query_count)))
    flat = padded.reshape(head_count, query_count * (width + 1))[:, : query_count * width]
    return jnp.sum(flat.reshape(head_count, query_count, width), axis=1)


def block_expo(queries, keys_block, first_query, first_key, offset_bias):
    query_count = queries.shape[1]
    key_count = keys_block.shape[1]
    query_pos = first_query + jnp.arange(query_count, dtype=jnp.int32)
    key_pos = first_key + jnp.arange(key_count, dtype=jnp.int32)
    pos_bias = skew_bias(offset_bias, first_query, first_key, query_count, key_count)
    raw_scores = jnp.einsum(
        "mqhd,mkhd->mhqk", queries, keys_block, preferred_element_type=jnp.float32
    )
    raw_scores = raw_scores * score_scale + pos_bias[None]
    allowed = key_pos[None, :] // BLOCK <= query_pos[:, None] // BLOCK
    return jnp.where(allowed[None, None], jnp.exp(raw_scores), 0.0)


def norm_back(norm_input, factor, gain_wide, grad_normed):
    scaled = grad_normed * gain_wide
    gain_grad = jnp.sum(grad_normed * norm_input * factor, axis=(0, 1))
    mean_term = jnp.mean(scaled * norm_input, axis=-1, keepdims=True)
    return (factor * scaled - norm_input * factor * factor * factor * mean_term, gain_grad)


def expert_inner(expert_rows, w_gate, w_up):
    gate_pre = jnp.dot(expert_rows, w_gate[0], preferred_element_type=jnp.float32)
    up_pre = jnp.dot(expert_rows, w_up[0], preferred_element_type=jnp.float32)
    return (gate_pre, up_pre)


def expert_forward(expert_rows, w_gate, w_up, w_down):
    gate_pre, up_pre = expert_inner(expert_rows, w_gate, w_up)
    hidden = (jax.nn.gelu(gate_pre, approximate=True) * up_pre).astype(jnp.bfloat16)
    result = jnp.dot(hidden, w_down[0], preferred_element_type=jnp.float32).astype(jnp.bfloat16)
    return (result, gate_pre, up_pre)


def expert_backward(expert_rows, gate_pre, up_pre, grad_out, w_gate, w_up, w_down):
    gelu_out, gelu_pull = jax.vjp(partial(jax.nn.gelu, approximate=True), gate_pre)
    hidden = (gelu_out * up_pre).astype(jnp.bfloat16)
    grad_hidden = lax.dot_general(
        grad_out, w_down[0], last_dims, preferred_element_type=jnp.float32
    )
    grad_gate = gelu_pull(grad_hidden * up_pre)[0].astype(jnp.bfloat16)
    grad_up = (grad_hidden * gelu_out).astype(jnp.bfloat16)
    down_grad = lax.dot_general(hidden, grad_out, first_dims, preferred_element_type=jnp.float32)
    gate_grad = lax.dot_general(
        expert_rows, grad_gate, first_dims, preferred_element_type=jnp.float32
    )
    up_grad = lax.dot_general(expert_rows, grad_up, first_dims, preferred_element_type=jnp.float32)
    grad_rows = lax.dot_general(grad_gate, w_gate[0], last_dims, preferred_element_type=jnp.float32)
    grad_rows = grad_rows + lax.dot_general(
        grad_up, w_up[0], last_dims, preferred_element_type=jnp.float32
    )
    return (grad_rows.astype(jnp.bfloat16), gate_grad[None], up_grad[None], down_grad[None])


def adamw_step(master, gradient, first_old, second_old):
    first_new = decay_rate * first_old + (1.0 - decay_rate) * gradient
    second_new = decay_rate * second_old + (1.0 - decay_rate) * gradient * gradient
    correct = 1.0 - decay_rate**STEP
    update = -learn_rate * (
        first_new / correct / (jnp.sqrt(second_new / correct) + eps_adam) + weight_decay * master
    )
    return (gradient, first_new, second_new, update)


def body(
    tokens,
    cotangent,
    bucket_ids,
    routes,
    qkv_master,
    out_master,
    router_master,
    gain_attn_master,
    gain_mix_master,
    table_master,
    gate_master,
    up_master,
    down_master,
    qkv_first,
    out_first,
    router_first,
    gain_attn_first,
    gain_mix_first,
    table_first,
    gate_first,
    up_first,
    down_first,
    qkv_second,
    out_second,
    router_second,
    gain_attn_second,
    gain_mix_second,
    table_second,
    gate_second,
    up_second,
    down_second,
):
    batch_count, tok_rows = (tokens.shape[0], tokens.shape[2])
    dense_copy = (
        lax.all_gather(qkv_master.astype(jnp.bfloat16), ("ctx", "exp"), axis=1, tiled=True),
        lax.all_gather(out_master.astype(jnp.bfloat16), ("ctx", "exp"), axis=0, tiled=True),
        lax.all_gather(router_master.astype(jnp.bfloat16), ("ctx", "exp"), axis=0, tiled=True),
        lax.all_gather(gain_attn_master.astype(jnp.bfloat16), ("ctx", "exp"), axis=0, tiled=True),
        lax.all_gather(gain_mix_master.astype(jnp.bfloat16), ("ctx", "exp"), axis=0, tiled=True),
        lax.all_gather(table_master.astype(jnp.bfloat16), ("ctx", "exp"), axis=0, tiled=True),
    )
    w_qkv, w_out, router_bf, gain_attn_bf, gain_mix_bf, table_bf = dense_copy
    w_gate, w_up, w_down = (
        lax.all_gather(gate_master.astype(jnp.bfloat16), "ctx", axis=1, tiled=True),
        lax.all_gather(up_master.astype(jnp.bfloat16), "ctx", axis=1, tiled=True),
        lax.all_gather(down_master.astype(jnp.bfloat16), "ctx", axis=1, tiled=True),
    )
    experts_all = router_bf.shape[1]
    capacity = 5 * tok_rows * TOP // (4 * experts_all)
    gain_attn = gain_attn_bf.astype(jnp.float32)
    gain_mix = gain_mix_bf.astype(jnp.float32)
    table_hb = table_bf.reshape(HEADS, -1).astype(jnp.float32)
    bucket_count = table_hb.shape[1]
    offset_bias = jnp.take(table_hb, bucket_ids, axis=1)
    offset_count = offset_bias.shape[1]
    router_wide = router_bf.astype(jnp.float32)
    cycle_size = lax.axis_size("ctx")
    ctx_place = lax.axis_index("ctx")
    first_query = ctx_place * tok_rows
    inputs = tokens.reshape(batch_count, tok_rows, D).astype(jnp.float32)
    factor_attn = lax.rsqrt(jnp.mean(inputs * inputs, axis=-1, keepdims=True) + eps_norm)
    normed = (inputs * factor_attn * gain_attn).astype(jnp.bfloat16)
    projected = jnp.einsum(
        "mtd,cde->cmte", normed, w_qkv, preferred_element_type=jnp.float32
    ).astype(jnp.bfloat16)
    queries = projected[0].reshape(batch_count, tok_rows, HEADS, HEAD_DIM)
    keys_own, values_own = (projected[1], projected[2])
    start_state = (
        jnp.zeros((batch_count, HEADS, tok_rows), jnp.float32),
        jnp.zeros((batch_count, tok_rows, HEADS, HEAD_DIM), jnp.float32),
    )
    keys_piece = lax.all_gather(keys_own, "ctx", axis=1, tiled=True)
    values_piece = lax.all_gather(values_own, "ctx", axis=1, tiled=True)
    key_count = keys_piece.shape[1]
    key_span = math.gcd(key_count, 512)

    def inner(turn_index, loop_state):
        row_total, summed = loop_state
        keys_block = lax.dynamic_slice_in_dim(
            keys_piece, turn_index * key_span, key_span, 1
        ).reshape(batch_count, key_span, HEADS, HEAD_DIM)
        values_block = lax.dynamic_slice_in_dim(
            values_piece, turn_index * key_span, key_span, 1
        ).reshape(batch_count, key_span, HEADS, HEAD_DIM)
        exp_scores = block_expo(
            queries, keys_block, first_query, turn_index * key_span, offset_bias
        )
        row_total = row_total + jnp.sum(exp_scores, axis=-1)
        summed = summed + jnp.einsum(
            "mhqk,mkhd->mqhd",
            exp_scores.astype(jnp.bfloat16),
            values_block,
            preferred_element_type=jnp.float32,
        )
        return (row_total, summed)

    row_total, summed = lax.fori_loop(0, key_count // key_span, inner, start_state)
    total_rows = jnp.transpose(row_total, (0, 2, 1))
    attended = summed / total_rows[:, :, :, None]
    attended_bf = attended.reshape(batch_count, tok_rows, D).astype(jnp.bfloat16)
    branch = jnp.dot(attended_bf, w_out, preferred_element_type=jnp.float32)
    hidden_state = inputs + branch
    factor_mix = lax.rsqrt(jnp.mean(hidden_state * hidden_state, axis=-1, keepdims=True) + eps_norm)
    normed_mix = hidden_state * factor_mix * gain_mix
    normed_bf = normed_mix.astype(jnp.bfloat16)
    logits = jnp.einsum("mtd,de->mte", normed_bf, router_bf, preferred_element_type=jnp.float32)
    router_probs = jax.nn.softmax(logits, axis=-1)
    route_rows = routes.reshape(batch_count, tok_rows, TOP)
    expert_ids = jnp.arange(experts_all, dtype=jnp.int32)
    picked = (route_rows[:, :, :, None] == expert_ids).astype(jnp.float32)
    chosen = jnp.sum(picked * router_probs[:, :, None, :], axis=-1)
    chosen_sum = jnp.sum(chosen, axis=-1, keepdims=True)
    gate_share = chosen / chosen_sum
    flat_routes = route_rows.reshape(batch_count, tok_rows * TOP)
    route_hits = (flat_routes[:, :, None] == expert_ids).astype(jnp.int32)
    before = jnp.cumsum(route_hits, axis=1) - route_hits
    slot_index = flat_routes * capacity + jnp.sum(before * route_hits, axis=-1)
    targets = expert_ids[:, None] * capacity + jnp.arange(capacity, dtype=jnp.int32)[None, :]
    dispatch = (slot_index[:, None, None, :] == targets[None, :, :, None]).astype(jnp.bfloat16)
    entries = jnp.repeat(normed_bf, TOP, axis=1)
    sent_rows = jnp.einsum(
        "mect,mtd->emcd", dispatch, entries, preferred_element_type=jnp.float32
    ).astype(jnp.bfloat16)
    dy_rows = cotangent.reshape(batch_count, tok_rows, D).astype(jnp.float32)
    scaled_dy = (
        (gate_share[:, :, :, None] * dy_rows[:, :, None, :])
        .astype(jnp.bfloat16)
        .reshape(batch_count, tok_rows * TOP, D)
    )
    sent_grads = jnp.einsum(
        "mect,mtd->emcd", dispatch, scaled_dy, preferred_element_type=jnp.float32
    ).astype(jnp.bfloat16)
    got_rows = lax.all_to_all(sent_rows, "exp", split_axis=0, concat_axis=0, tiled=True)
    flat_rows = got_rows.reshape(-1, D)
    out_rows, gate_unused, up_unused = expert_forward(flat_rows, w_gate, w_up, w_down)
    back_out = lax.all_to_all(
        out_rows.reshape(got_rows.shape), "exp", split_axis=0, concat_axis=0, tiled=True
    )
    got_grads = lax.all_to_all(sent_grads, "exp", split_axis=0, concat_axis=0, tiled=True)
    again_gate, again_up, again_down = (
        lax.all_gather(gate_master.astype(jnp.bfloat16), "ctx", axis=1, tiled=True),
        lax.all_gather(up_master.astype(jnp.bfloat16), "ctx", axis=1, tiled=True),
        lax.all_gather(down_master.astype(jnp.bfloat16), "ctx", axis=1, tiled=True),
    )
    gate_pre, up_pre = expert_inner(flat_rows, again_gate, again_up)
    grad_rows, gate_grad, up_grad, down_grad = expert_backward(
        flat_rows, gate_pre, up_pre, got_grads.reshape(-1, D), again_gate, again_up, again_down
    )
    back_grad = lax.all_to_all(
        grad_rows.reshape(got_rows.shape), "exp", split_axis=0, concat_axis=0, tiled=True
    )
    returned = jnp.einsum(
        "mect,emcd->mtd", dispatch, back_out, preferred_element_type=jnp.float32
    ).reshape(batch_count, tok_rows, TOP, D)
    mix_out = jnp.sum(gate_share[:, :, :, None] * returned, axis=2)
    output = (hidden_state + mix_out).astype(jnp.bfloat16)
    grad_entries = jnp.einsum(
        "mect,emcd->mtd", dispatch, back_grad, preferred_element_type=jnp.float32
    ).reshape(batch_count, tok_rows, TOP, D)
    grad_gates = jnp.sum(dy_rows[:, :, None, :] * returned, axis=-1)
    grad_chosen = grad_gates / chosen_sum - jnp.sum(grad_gates * chosen, axis=-1, keepdims=True) / (
        chosen_sum * chosen_sum
    )
    grad_probs = jnp.sum(grad_chosen[:, :, :, None] * picked, axis=2)
    grad_logits = router_probs * (
        grad_probs - jnp.sum(router_probs * grad_probs, axis=-1, keepdims=True)
    )
    router_grad = jnp.einsum(
        "mtd,mte->de", normed_bf.astype(jnp.float32), grad_logits, precision=highest
    )
    grad_normed = jnp.sum(grad_entries, axis=2) + jnp.einsum(
        "mte,de->mtd", grad_logits, router_wide, precision=highest
    )
    grad_hidden, gain_mix_grad = norm_back(hidden_state, factor_mix, gain_mix, grad_normed)
    grad_hidden = grad_hidden + dy_rows
    grad_branch = grad_hidden.astype(jnp.bfloat16)
    out_grad = jnp.einsum(
        "mtd,mte->de", attended_bf, grad_branch, preferred_element_type=jnp.float32
    )
    grad_attended = jnp.einsum(
        "mte,de->mtd", grad_branch, w_out, preferred_element_type=jnp.float32
    ).astype(jnp.bfloat16)
    grad_attended = grad_attended.reshape(batch_count, tok_rows, HEADS, HEAD_DIM).astype(
        jnp.float32
    )
    grad_summed = (grad_attended / total_rows[:, :, :, None]).astype(jnp.bfloat16)
    total_shift = -jnp.sum(grad_attended * attended, axis=-1) / total_rows
    total_shift = jnp.transpose(total_shift, (0, 2, 1))

    def key_block_grads(
        keys_block, values_block, grad_keys, grad_values, grad_queries, offset_grad, first_row
    ):
        keys_heads = keys_block.reshape(batch_count, tok_rows, HEADS, HEAD_DIM)
        values_heads = values_block.reshape(batch_count, tok_rows, HEADS, HEAD_DIM)
        exp_scores = block_expo(queries, keys_heads, first_query, first_row, offset_bias)
        grad_probs_kv = jnp.einsum(
            "mqhd,mkhd->mhqk", grad_summed, values_heads, preferred_element_type=jnp.float32
        )
        score_grad = (exp_scores * (grad_probs_kv + total_shift[:, :, :, None])).astype(
            jnp.bfloat16
        )
        grad_queries = (
            grad_queries
            + jnp.einsum(
                "mhqk,mkhd->mqhd", score_grad, keys_heads, preferred_element_type=jnp.float32
            )
            * score_scale
        )
        key_term = (
            jnp.einsum("mhqk,mqhd->mkhd", score_grad, queries, preferred_element_type=jnp.float32)
            * score_scale
        )
        value_term = jnp.einsum(
            "mhqk,mqhd->mkhd",
            exp_scores.astype(jnp.bfloat16),
            grad_summed,
            preferred_element_type=jnp.float32,
        )
        grad_keys = grad_keys + key_term.reshape(batch_count, tok_rows, D)
        grad_values = grad_values + value_term.reshape(batch_count, tok_rows, D)
        pair_grad = jnp.sum(score_grad.astype(jnp.float32), axis=0)
        diagonal = diagonal_sums(pair_grad, tok_rows, tok_rows)
        start = window_start(first_query, first_row, tok_rows, offset_bias)
        width = diagonal.shape[1]
        current = lax.dynamic_slice_in_dim(offset_grad, start, width, 1)
        offset_grad = lax.dynamic_update_slice_in_dim(offset_grad, current + diagonal, start, 1)
        return (grad_keys, grad_values, grad_queries, offset_grad)

    def pass_grads(grad_keys, grad_values):
        return passed_along((grad_keys, grad_values), "ctx", 1)

    zero_rows = jnp.zeros((batch_count, tok_rows, D), jnp.float32)
    zero_queries = jnp.zeros((batch_count, tok_rows, HEADS, HEAD_DIM), jnp.float32)
    zero_offsets = jnp.zeros((HEADS, offset_count), jnp.float32)

    def cycle_turn(turn_index, loop_state):
        keys_block, values_block, grad_keys, grad_values, grad_queries, offset_grad = loop_state
        first_row = (ctx_place - turn_index) % cycle_size * tok_rows
        grad_keys, grad_values, grad_queries, offset_grad = key_block_grads(
            keys_block, values_block, grad_keys, grad_values, grad_queries, offset_grad, first_row
        )
        grad_keys, grad_values = pass_grads(grad_keys, grad_values)
        keys_block, values_block = passed_along((keys_block, values_block), "ctx", 1)
        return (keys_block, values_block, grad_keys, grad_values, grad_queries, offset_grad)

    cycle_start = (keys_own, values_own, zero_rows, zero_rows, zero_queries, zero_offsets)
    keys_block, values_block, grad_keys, grad_values, grad_queries, offset_grad = lax.fori_loop(
        0, cycle_size - 1, cycle_turn, cycle_start
    )
    last_row = (ctx_place - (cycle_size - 1)) % cycle_size * tok_rows
    grad_keys, grad_values, grad_queries, offset_grad = key_block_grads(
        keys_block, values_block, grad_keys, grad_values, grad_queries, offset_grad, last_row
    )
    grad_keys, grad_values = pass_grads(grad_keys, grad_values)
    bucket_hits = (
        bucket_ids[:, None] == jnp.arange(bucket_count, dtype=jnp.int32)[None, :]
    ).astype(jnp.float32)
    table_grad = jnp.dot(offset_grad, bucket_hits, precision=highest)
    grad_projected = jnp.stack(
        [grad_queries.reshape(batch_count, tok_rows, D), grad_keys, grad_values]
    ).astype(jnp.bfloat16)
    qkv_grad = jnp.einsum(
        "mtd,cmte->cde", normed, grad_projected, preferred_element_type=jnp.float32
    )
    grad_normed_attn = jnp.einsum(
        "cmte,cde->mtd", grad_projected, w_qkv, preferred_element_type=jnp.float32
    )
    grad_inputs, gain_attn_grad = norm_back(inputs, factor_attn, gain_attn, grad_normed_attn)
    grad_inputs = grad_inputs + grad_hidden
    dense_sums = (
        lax.psum_scatter(qkv_grad, ("ctx", "exp"), scatter_dimension=1, tiled=True),
        lax.psum_scatter(out_grad, ("ctx", "exp"), scatter_dimension=0, tiled=True),
        lax.psum_scatter(router_grad, ("ctx", "exp"), scatter_dimension=0, tiled=True),
        lax.psum_scatter(gain_attn_grad, ("ctx", "exp"), scatter_dimension=0, tiled=True),
        lax.psum_scatter(gain_mix_grad, ("ctx", "exp"), scatter_dimension=0, tiled=True),
        lax.psum_scatter(table_grad.reshape(-1), ("ctx", "exp"), scatter_dimension=0, tiled=True),
    )
    expert_sums = (
        lax.psum_scatter(
            gate_grad.astype(jnp.bfloat16), "ctx", scatter_dimension=1, tiled=True
        ).astype(jnp.float32),
        lax.psum_scatter(
            up_grad.astype(jnp.bfloat16), "ctx", scatter_dimension=1, tiled=True
        ).astype(jnp.float32),
        lax.psum_scatter(
            down_grad.astype(jnp.bfloat16), "ctx", scatter_dimension=1, tiled=True
        ).astype(jnp.float32),
    )
    gradients = tuple(dense_sums) + tuple(expert_sums)
    masters = (
        qkv_master,
        out_master,
        router_master,
        gain_attn_master,
        gain_mix_master,
        table_master,
        gate_master,
        up_master,
        down_master,
    )
    firsts = (
        qkv_first,
        out_first,
        router_first,
        gain_attn_first,
        gain_mix_first,
        table_first,
        gate_first,
        up_first,
        down_first,
    )
    seconds = (
        qkv_second,
        out_second,
        router_second,
        gain_attn_second,
        gain_mix_second,
        table_second,
        gate_second,
        up_second,
        down_second,
    )
    results = [
        adamw_step(master, gradient, first_old, second_old)
        for master, gradient, first_old, second_old in zip(masters, gradients, firsts, seconds)
    ]
    qkv_g, qkv_first_new, qkv_second_new, qkv_update = results[0]
    out_g, out_first_new, out_second_new, out_update = results[1]
    router_g, router_first_new, router_second_new, router_update = results[2]
    gain_attn_g, gain_attn_first_new, gain_attn_second_new, gain_attn_update = results[3]
    gain_mix_g, gain_mix_first_new, gain_mix_second_new, gain_mix_update = results[4]
    table_g, table_first_new, table_second_new, table_update = results[5]
    gate_g, gate_first_new, gate_second_new, gate_update = results[6]
    up_g, up_first_new, up_second_new, up_update = results[7]
    down_g, down_first_new, down_second_new, down_update = results[8]
    return (
        output.reshape(tokens.shape),
        grad_inputs.reshape(tokens.shape),
        qkv_g,
        out_g,
        router_g,
        gain_attn_g,
        gain_mix_g,
        table_g,
        gate_g,
        up_g,
        down_g,
        qkv_first_new,
        out_first_new,
        router_first_new,
        gain_attn_first_new,
        gain_mix_first_new,
        table_first_new,
        gate_first_new,
        up_first_new,
        down_first_new,
        qkv_second_new,
        out_second_new,
        router_second_new,
        gain_attn_second_new,
        gain_mix_second_new,
        table_second_new,
        gate_second_new,
        up_second_new,
        down_second_new,
        qkv_update,
        out_update,
        router_update,
        gain_attn_update,
        gain_mix_update,
        table_update,
        gate_update,
        up_update,
        down_update,
    )


def solution(mesh):
    placed = (
        P(None, "exp", "ctx", None),
        P(None, "exp", "ctx", None),
        P(),
        P(None, "exp", "ctx", None),
        P(None, ("ctx", "exp"), None),
        P(("ctx", "exp"), None),
        P(("ctx", "exp"), None),
        P(("ctx", "exp")),
        P(("ctx", "exp")),
        P(("ctx", "exp")),
        P("exp", "ctx", None),
        P("exp", "ctx", None),
        P("exp", "ctx", None),
        P(None, ("ctx", "exp"), None),
        P(("ctx", "exp"), None),
        P(("ctx", "exp"), None),
        P(("ctx", "exp")),
        P(("ctx", "exp")),
        P(("ctx", "exp")),
        P("exp", "ctx", None),
        P("exp", "ctx", None),
        P("exp", "ctx", None),
        P(None, ("ctx", "exp"), None),
        P(("ctx", "exp"), None),
        P(("ctx", "exp"), None),
        P(("ctx", "exp")),
        P(("ctx", "exp")),
        P(("ctx", "exp")),
        P("exp", "ctx", None),
        P("exp", "ctx", None),
        P("exp", "ctx", None),
    )
    return jax.shard_map(
        body,
        mesh=mesh,
        in_specs=placed,
        out_specs=(
            P(None, "exp", "ctx", None),
            P(None, "exp", "ctx", None),
            P(None, ("ctx", "exp"), None),
            P(("ctx", "exp"), None),
            P(("ctx", "exp"), None),
            P(("ctx", "exp")),
            P(("ctx", "exp")),
            P(("ctx", "exp")),
            P("exp", "ctx", None),
            P("exp", "ctx", None),
            P("exp", "ctx", None),
            P(None, ("ctx", "exp"), None),
            P(("ctx", "exp"), None),
            P(("ctx", "exp"), None),
            P(("ctx", "exp")),
            P(("ctx", "exp")),
            P(("ctx", "exp")),
            P("exp", "ctx", None),
            P("exp", "ctx", None),
            P("exp", "ctx", None),
            P(None, ("ctx", "exp"), None),
            P(("ctx", "exp"), None),
            P(("ctx", "exp"), None),
            P(("ctx", "exp")),
            P(("ctx", "exp")),
            P(("ctx", "exp")),
            P("exp", "ctx", None),
            P("exp", "ctx", None),
            P("exp", "ctx", None),
            P(None, ("ctx", "exp"), None),
            P(("ctx", "exp"), None),
            P(("ctx", "exp"), None),
            P(("ctx", "exp")),
            P(("ctx", "exp")),
            P(("ctx", "exp")),
            P("exp", "ctx", None),
            P("exp", "ctx", None),
            P("exp", "ctx", None),
        ),
        check_vma=False,
    )
```

profile of v0, /device:TPU:5, one launch (start us, length us, event | category | flops | bytes accessed | tf_op | source)
XLA Modules:
  0.0 2217.4 jit_solution(734634548502726985)
XLA Ops:
  11.6 40.3 %all-reduce.13 = (bf16[512]{0:T(512)(128)(2,1)S(1)}, bf16[1024]{0:T(1024)(128)(2,1)S(1)}, bf16[1024]{0:T(1024)(128)(2,1)S(1)}) all-reduce(bf16[512]{0:T(512)(128)(2,1)S(1)} %dynamic-update-slice.1, bf16[1024]{0:T(1024)(128)(2,1)S(1)} %dynamic-update-slice, ...), channel_id=1, replica_groups=mesh['ctx'=8,'exp'=4] {'ctx','exp'}, use_global_device_ids=true, to_apply=%add.6 | all-reduce | flops 2560 | bytes 10240
  53.2 29.3 %all-gather.11.cloned.1.call-done = bf16[3,1024,1024]{2,1,0:T(8,128)(2,1)} async-done(((bf16[3,32,1024]{2,1,0:T(8,128)(2,1)}), bf16[3,1024,1024]{2,1,0:T(8,128)(2,1)}) %all-gather.11.cloned.1.call-update) | async-done | bytes 6291472 | tf_op jit(solution)/shard_map/all_gather | solution.py:159
  104.9 37.9 %all-gather.2 = bf16[32,32,4]{1,2,0:T(4,128)(2,1)S(1)} all-gather(bf16[1,32,4]{1,2,0:T(4,128)(2,1)S(1)} %convert_bitcast_fusion.5), channel_id=1, replica_groups=mesh['ctx'=8,'exp'=4] {'ctx','exp'}, dimensions={0}, use_global_device_ids=true | all-gather | bytes 8448 | tf_op jit(solution)/shard_map/all_gather | solution.py:161
  159.0 74.1 %all-gather.21.cloned.1.call-done = bf16[1,2,1024,1024]{3,2,0,1:T(8,128)(2,1)} async-done(((bf16[1,2,128,1024]{3,2,0,1:T(8,128)(2,1)}), bf16[1,2,1024,1024]{3,2,0,1:T(8,128)(2,1)}) %all-gather.21.cloned.1.call-update) | async-done | bytes 4194320 | tf_op jit(solution)/shard_map/all_gather | solution.py:196
  233.1 116.0 %while.50 = (s32[]{:T(128)}, f32[2,16,128]{2,1,0:T(8,128)S(1)}, f32[2,128,16,64]{1,3,2,0:T(8,128)}, s32[]{:T(128)}, bf16[2,1024,1024]{2,1,0:T(8,128)(2,1)}, /*in...) while((s32[]{:T(128)}, f32[2,16,128]{2,1,0:T(8,128)S(1)}, ...), condition=%wide.region_3.4_spmd.clone, body=%wide.region_1.3_spmd.clone.sunk | while | flops 554252288 | bytes 113062984 | solution.py:221
  411.5 66.3 %all-gather.19.cloned.1.call-done = bf16[1,2816,1024]{2,1,0:T(8,128)(2,1)} async-done(((bf16[1,352,1024]{2,1,0:T(8,128)(2,1)}), bf16[1,2816,1024]{2,1,0:T(8,128)(2,1)}) %all-gather.19.cloned.1.call-update) | async-done | bytes 5767184 | tf_op jit(solution)/shard_map/all_gather | solution.py:170
  487.7 83.4 %all-gather.15.cloned.1.call-done = bf16[1,1024,2816]{2,1,0:T(8,128)(2,1)} async-done(((bf16[1,128,2816]{2,1,0:T(8,128)(2,1)}), bf16[1,1024,2816]{2,1,0:T(8,128)(2,1)}) %all-gather.15.cloned.1.call-update) | async-done | bytes 5767184 | tf_op jit(solution)/shard_map/all_gather | solution.py:168
  571.1 16.8 fusion.32
  656.6 618.0 %while.51 = (s32[]{:T(128)}, bf16[2,128,1024]{1,2,0:T(8,128)(2,1)}, bf16[2,128,1024]{1,2,0:T(8,128)(2,1)}, f32[2,128,1024]{1,2,0:T(8,128)}, f32[2,128,1024]{1,2,...) while((s32[]{:T(128)}, bf16[2,128,1024]{1,2,0:T(8,128)(2,1)}, ...), condition=%wide.region_23.24_spmd.clone, body=%wide.region_20.23_spmd.clone.sunk | while | flops 342116352 | bytes 89761912 | solution.py:371
  693.6 42.7 %collective-permute-done = bf16[2,128,1024]{1,2,0:T(8,128)(2,1)} collective-permute-done((bf16[2,128,1024]{1,2,0:T(8,128)(2,1)}, bf16[2,128,1024]{1,2,0:T(8,128)(2,1)}, u32[]{:S(2)}, u32[]{:S(2)}) %collective-permute-start) | collective-permute-done | bytes 524320 | tf_op jit(solution)/shard_map/while/body/eval_jaxpr/ppermute | solution.py:31
  782.8 43.4 %collective-permute-done = bf16[2,128,1024]{1,2,0:T(8,128)(2,1)} collective-permute-done((bf16[2,128,1024]{1,2,0:T(8,128)(2,1)}, bf16[2,128,1024]{1,2,0:T(8,128)(2,1)}, u32[]{:S(2)}, u32[]{:S(2)}) %collective-permute-start) | collective-permute-done | bytes 524320 | tf_op jit(solution)/shard_map/while/body/eval_jaxpr/ppermute | solution.py:31
  871.1 44.3 %collective-permute-done = bf16[2,128,1024]{1,2,0:T(8,128)(2,1)} collective-permute-done((bf16[2,128,1024]{1,2,0:T(8,128)(2,1)}, bf16[2,128,1024]{1,2,0:T(8,128)(2,1)}, u32[]{:S(2)}, u32[]{:S(2)}) %collective-permute-start) | collective-permute-done | bytes 524320 | tf_op jit(solution)/shard_map/while/body/eval_jaxpr/ppermute | solution.py:31
  959.9 43.7 %collective-permute-done = bf16[2,128,1024]{1,2,0:T(8,128)(2,1)} collective-permute-done((bf16[2,128,1024]{1,2,0:T(8,128)(2,1)}, bf16[2,128,1024]{1,2,0:T(8,128)(2,1)}, u32[]{:S(2)}, u32[]{:S(2)}) %collective-permute-start) | collective-permute-done | bytes 524320 | tf_op jit(solution)/shard_map/while/body/eval_jaxpr/ppermute | solution.py:31
  1048.2 42.8 %collective-permute-done = bf16[2,128,1024]{1,2,0:T(8,128)(2,1)} collective-permute-done((bf16[2,128,1024]{1,2,0:T(8,128)(2,1)}, bf16[2,128,1024]{1,2,0:T(8,128)(2,1)}, u32[]{:S(2)}, u32[]{:S(2)}) %collective-permute-start) | collective-permute-done | bytes 524320 | tf_op jit(solution)/shard_map/while/body/eval_jaxpr/ppermute | solution.py:31
  1135.6 41.9 %collective-permute-done = bf16[2,128,1024]{1,2,0:T(8,128)(2,1)} collective-permute-done((bf16[2,128,1024]{1,2,0:T(8,128)(2,1)}, bf16[2,128,1024]{1,2,0:T(8,128)(2,1)}, u32[]{:S(2)}, u32[]{:S(2)}) %collective-permute-start) | collective-permute-done | bytes 524320 | tf_op jit(solution)/shard_map/while/body/eval_jaxpr/ppermute | solution.py:31
  1222.1 41.1 %collective-permute-done = bf16[2,128,1024]{1,2,0:T(8,128)(2,1)} collective-permute-done((bf16[2,128,1024]{1,2,0:T(8,128)(2,1)}, bf16[2,128,1024]{1,2,0:T(8,128)(2,1)}, u32[]{:S(2)}, u32[]{:S(2)}) %collective-permute-start) | collective-permute-done | bytes 524320 | tf_op jit(solution)/shard_map/while/body/eval_jaxpr/ppermute | solution.py:31
  1316.6 18.4 copy.269
  1388.1 43.6 %reduce-scatter.16.cloned.1.call-done = f32[32,4]{1,0:T(8,128)} async-done(((f32[1024,4]{1,0:T(8,128)}), f32[32,4]{1,0:T(8,128)}) %reduce-scatter.16.cloned.1.call-update) | async-done | bytes 528
  1439.4 48.3 %all-reduce.12 = (f32[1024]{0:T(1024)S(1)}, f32[1024]{0:T(1024)S(1)}, f32[512]{0:T(512)S(1)}) all-reduce(f32[1024]{0:T(1024)S(1)} %get-tuple-element.1155, f32[1024]{0:T(1024)S(1)} %copy-done.48, f32[512]{0:T(512)S(1)} %reshape.774), channel_id=7, replica_groups=mesh['ctx'=8,'exp'=4] {'ctx','exp'}, use_global_device_ids=true, to_apply=%region_29.30.clone | all-reduce | flops 2560 | bytes 20480
  1492.4 230.5 %all-reduce.16.cloned.1.call-done = f32[3,1024,1024]{2,0,1:T(4,128)} async-done(((f32[3,1024,1024]{2,0,1:T(4,128)}), f32[3,1024,1024]{2,0,1:T(4,128)}) %all-reduce.16.cloned.1.call-update) | async-done | bytes 12582928
  1725.6 132.5 %reduce-scatter.8.cloned.1.call-done = f32[32,1024]{1,0:T(8,128)} async-done(((f32[1024,1024]{1,0:T(8,128)}), f32[32,1024]{1,0:T(8,128)}) %reduce-scatter.8.cloned.1.call-update) | async-done | bytes 131088 | tf_op jit(solution)/shard_map/reduce_scatter | solution.py:396
  1859.8 118.6 %reduce-scatter.12.cloned.1.call-done = bf16[1,128,2816]{2,1,0:T(8,128)(2,1)} async-done(((bf16[1,1024,2816]{2,1,0:T(8,128)(2,1)}), bf16[1,128,2816]{2,1,0:T(8,128)(2,1)}) %reduce-scatter.12.cloned.1.call-update) | async-done | bytes 720912 | tf_op jit(solution)/shard_map/reduce_scatter | solution.py:406
  1983.2 108.6 %reduce-scatter.10.cloned.1.call-done = bf16[1,128,2816]{2,1,0:T(8,128)(2,1)} async-done(((bf16[1,1024,2816]{2,1,0:T(8,128)(2,1)}), bf16[1,128,2816]{2,1,0:T(8,128)(2,1)}) %reduce-scatter.10.cloned.1.call-update) | async-done | bytes 720912 | tf_op jit(solution)/shard_map/reduce_scatter | solution.py:403
  2096.7 108.8 %reduce-scatter.14.cloned.1.call-done = bf16[1,352,1024]{2,1,0:T(8,128)(2,1)} async-done(((bf16[1,2816,1024]{2,1,0:T(8,128)(2,1)}), bf16[1,352,1024]{2,1,0:T(8,128)(2,1)}) %reduce-scatter.14.cloned.1.call-update) | async-done | bytes 720912 | tf_op jit(solution)/shard_map/reduce_scatter | solution.py:409
  (649 shorter events, 732.6 us)
Async XLA Ops:
  7.2 75.3 %all-gather.11.cloned.1.call-start = ((), (), s32[]{:S(2)}) async-start(), calls=%async_computation.9 | async-start | bytes 6488064 | tf_op jit(solution)/shard_map/all_gather | solution.py:159
  9.0 150.0 %all-gather.23.cloned.1.call-start = ((), (), s32[]{:S(2)}) async-start(), calls=%async_computation.19 | async-start | bytes 4718592 | tf_op jit(solution)/shard_map/all_gather | solution.py:197
  89.0 144.1 %all-gather.21.cloned.1.call-start = ((), (), s32[]{:S(2)}) async-start(), calls=%async_computation.18 | async-start | bytes 4718592 | tf_op jit(solution)/shard_map/all_gather | solution.py:196
  89.7 260.8 %all-gather.13.cloned.1.call-start = ((), (), s32[]{:S(2)}) async-start(), calls=%async_computation.10 | async-start | bytes 2162688 | tf_op jit(solution)/shard_map/all_gather | solution.py:160
  90.4 311.2 %all-gather.17.cloned.1.call-start = ((), (), s32[]{:S(2)}) async-start(), calls=%async_computation.12 | async-start | bytes 6488064 | tf_op jit(solution)/shard_map/all_gather | solution.py:169
  91.5 386.4 %all-gather.19.cloned.1.call-start = ((), (), s32[]{:S(2)}) async-start(), calls=%async_computation.13 | async-start | bytes 6488064 | tf_op jit(solution)/shard_map/all_gather | solution.py:170
  92.5 478.6 %all-gather.15.cloned.1.call-start = ((), (), s32[]{:S(2)}) async-start(), calls=%async_computation.11 | async-start | bytes 6488064 | tf_op jit(solution)/shard_map/all_gather | solution.py:168
  379.1 98.7 %all-to-all-start.2 = ((bf16[4,2,80,1024]{3,2,1,0:T(8,128)(2,1)}), bf16[4,2,80,1024]{3,2,1,0:T(8,128)(2,1)}, u32[]{:S(2)}, u32[]{:S(2)}) async-start(bf16[4,2,80,1024]{3,2,1,0:T(8,128)(2,1)} %copy.254), calls=%async_computation.2 | async-start | bytes 2621440 | tf_op jit(solution)/shard_map/all_to_all | solution.py:263
  621.1 810.6 %reduce-scatter.16.cloned.1.call-start = ((), (), s32[]{:S(2)}) async-start(), calls=%async_computation.20 | async-start | bytes 540672
  675.5 72.1 %collective-permute-start.2 = (f32[2,128,1024]{1,2,0:T(8,128)}, f32[2,128,1024]{1,2,0:T(8,128)}, u32[]{:S(2)}, u32[]{:S(2)}) collective-permute-start(f32[2,128,1024]{1,2,0:T(8,128)} %bitcast_add_fusion.5), channel_id=1, source_target_pairs={{0,4},{4,8},{8,12},{12,16},{16,20},{20,24},{24,28},{28,0},{1,5},{5... | collective-permute-start | bytes 3145736 | tf_op jit(solution)/shard_map/while/body/eval_jaxpr/ppermute | solution.py:31
  678.5 69.1 %collective-permute-start.3 = (f32[2,128,1024]{1,2,0:T(8,128)}, f32[2,128,1024]{1,2,0:T(8,128)}, u32[]{:S(2)}, u32[]{:S(2)}) collective-permute-start(f32[2,128,1024]{1,2,0:T(8,128)} %bitcast_add_fusion.6), channel_id=1, source_target_pairs={{0,4},{4,8},{8,12},{12,16},{16,20},{20,24},{24,28},{28,0},{1,5},{5... | collective-permute-start | bytes 3145736 | tf_op jit(solution)/shard_map/while/body/eval_jaxpr/ppermute | solution.py:31
  679.9 67.7 %collective-permute-start.1 = (bf16[2,128,1024]{1,2,0:T(8,128)(2,1)}, bf16[2,128,1024]{1,2,0:T(8,128)(2,1)}, u32[]{:S(2)}, u32[]{:S(2)}) collective-permute-start(bf16[2,128,1024]{1,2,0:T(8,128)(2,1)} %copy.334), channel_id=1, source_target_pairs={{0,4},{4,8},{8,12},{12,16},{16,20},{20,24},{24,28},{28,0},{1,5},{5... | collective-permute-start | bytes 1572872 | tf_op jit(solution)/shard_map/while/body/eval_jaxpr/ppermute | solution.py:31
  766.3 71.2 %collective-permute-start.2 = (f32[2,128,1024]{1,2,0:T(8,128)}, f32[2,128,1024]{1,2,0:T(8,128)}, u32[]{:S(2)}, u32[]{:S(2)}) collective-permute-start(f32[2,128,1024]{1,2,0:T(8,128)} %bitcast_add_fusion.5), channel_id=1, source_target_pairs={{0,4},{4,8},{8,12},{12,16},{16,20},{20,24},{24,28},{28,0},{1,5},{5... | collective-permute-start | bytes 3145736 | tf_op jit(solution)/shard_map/while/body/eval_jaxpr/ppermute | solution.py:31
  769.0 68.5 %collective-permute-start.3 = (f32[2,128,1024]{1,2,0:T(8,128)}, f32[2,128,1024]{1,2,0:T(8,128)}, u32[]{:S(2)}, u32[]{:S(2)}) collective-permute-start(f32[2,128,1024]{1,2,0:T(8,128)} %bitcast_add_fusion.6), channel_id=1, source_target_pairs={{0,4},{4,8},{8,12},{12,16},{16,20},{20,24},{24,28},{28,0},{1,5},{5... | collective-permute-start | bytes 3145736 | tf_op jit(solution)/shard_map/while/body/eval_jaxpr/ppermute | solution.py:31
  769.0 68.5 %collective-permute-start.1 = (bf16[2,128,1024]{1,2,0:T(8,128)(2,1)}, bf16[2,128,1024]{1,2,0:T(8,128)(2,1)}, u32[]{:S(2)}, u32[]{:S(2)}) collective-permute-start(bf16[2,128,1024]{1,2,0:T(8,128)(2,1)} %copy.334), channel_id=1, source_target_pairs={{0,4},{4,8},{8,12},{12,16},{16,20},{20,24},{24,28},{28,0},{1,5},{5... | collective-permute-start | bytes 1572872 | tf_op jit(solution)/shard_map/while/body/eval_jaxpr/ppermute | solution.py:31
  856.3 70.4 %collective-permute-start.2 = (f32[2,128,1024]{1,2,0:T(8,128)}, f32[2,128,1024]{1,2,0:T(8,128)}, u32[]{:S(2)}, u32[]{:S(2)}) collective-permute-start(f32[2,128,1024]{1,2,0:T(8,128)} %bitcast_add_fusion.5), channel_id=1, source_target_pairs={{0,4},{4,8},{8,12},{12,16},{16,20},{20,24},{24,28},{28,0},{1,5},{5... | collective-permute-start | bytes 3145736 | tf_op jit(solution)/shard_map/while/body/eval_jaxpr/ppermute | solution.py:31
  945.3 69.5 %collective-permute-start.2 = (f32[2,128,1024]{1,2,0:T(8,128)}, f32[2,128,1024]{1,2,0:T(8,128)}, u32[]{:S(2)}, u32[]{:S(2)}) collective-permute-start(f32[2,128,1024]{1,2,0:T(8,128)} %bitcast_add_fusion.5), channel_id=1, source_target_pairs={{0,4},{4,8},{8,12},{12,16},{16,20},{20,24},{24,28},{28,0},{1,5},{5... | collective-permute-start | bytes 3145736 | tf_op jit(solution)/shard_map/while/body/eval_jaxpr/ppermute | solution.py:31
  1033.6 68.6 %collective-permute-start.2 = (f32[2,128,1024]{1,2,0:T(8,128)}, f32[2,128,1024]{1,2,0:T(8,128)}, u32[]{:S(2)}, u32[]{:S(2)}) collective-permute-start(f32[2,128,1024]{1,2,0:T(8,128)} %bitcast_add_fusion.5), channel_id=1, source_target_pairs={{0,4},{4,8},{8,12},{12,16},{16,20},{20,24},{24,28},{28,0},{1,5},{5... | collective-permute-start | bytes 3145736 | tf_op jit(solution)/shard_map/while/body/eval_jaxpr/ppermute | solution.py:31
  1121.0 67.8 %collective-permute-start.2 = (f32[2,128,1024]{1,2,0:T(8,128)}, f32[2,128,1024]{1,2,0:T(8,128)}, u32[]{:S(2)}, u32[]{:S(2)}) collective-permute-start(f32[2,128,1024]{1,2,0:T(8,128)} %bitcast_add_fusion.5), channel_id=1, source_target_pairs={{0,4},{4,8},{8,12},{12,16},{16,20},{20,24},{24,28},{28,0},{1,5},{5... | collective-permute-start | bytes 3145736 | tf_op jit(solution)/shard_map/while/body/eval_jaxpr/ppermute | solution.py:31
  1298.5 424.5 %all-reduce.16.cloned.1.call-start = ((), (), s32[]{:S(2)}) async-start(), calls=%async_computation.21 | async-start | bytes 33554432
  1335.1 523.0 %reduce-scatter.8.cloned.1.call-start = ((), (), s32[]{:S(2)}) async-start(), calls=%async_computation.14 | async-start | bytes 4325376 | tf_op jit(solution)/shard_map/reduce_scatter | solution.py:396
  1339.1 639.3 %reduce-scatter.12.cloned.1.call-start = ((), (), s32[]{:S(2)}) async-start(), calls=%async_computation.16 | async-start | bytes 6488064 | tf_op jit(solution)/shard_map/reduce_scatter | solution.py:406
  1349.2 742.7 %reduce-scatter.10.cloned.1.call-start = ((), (), s32[]{:S(2)}) async-start(), calls=%async_computation.15 | async-start | bytes 6488064 | tf_op jit(solution)/shard_map/reduce_scatter | solution.py:403
  1358.8 846.7 %reduce-scatter.14.cloned.1.call-start = ((), (), s32[]{:S(2)}) async-start(), calls=%async_computation.17 | async-start | bytes 6488064 | tf_op jit(solution)/shard_map/reduce_scatter | solution.py:409
  (115 other events, 6429.2 us)
Sparse Core Ops, SparseCore 0:
  11.5 70.8 all-gather.10
  89.1 69.8 all-gather.22
  161.8 71.2 all-gather.20
  236.4 56.3 all-gather.12
  295.4 89.2 all-gather.16
  387.3 90.4 all-gather.18
  480.6 90.4 all-gather.14
  1298.6 133.1 reduce-scatter.15
  1437.8 285.0 all-reduce.15
  1725.6 132.4 reduce-scatter.7
  1861.8 116.5 reduce-scatter.11
  1981.9 109.9 reduce-scatter.9
  2095.5 109.9 reduce-scatter.13
where the time goes:
time: 2230 us; the launch traced here: 2220 us
  waiting for transfers between devices  1410 us (63%)
  local copies, waits for them, and re-layouts  307 us (14%)
  matrix products  218 us (10%)
  blocking collectives  127 us (6%)
  other arithmetic  91.8 us (4%)
  starting transfers between devices  32.7 us (1%)
    ppermute x30, waiting for transfers between devices, passed_along(): return lax.ppermute(value, axis, pairs)  389 us
    unnamed x15, waiting for transfers between devices  275 us
    reduce_scatter x1, waiting for transfers between devices, body(): lax.psum_scatter(out_grad, ('ctx', 'exp'), scatter_dimension=0, tiled=True)  133 us
    reduce_scatter x1, waiting for transfers between devices, body(): lax.psum_scatter(up_grad.astype(jnp.bfloat16), 'ctx', scatter_dimension=1...  119 us
    reduce_scatter x1, waiting for transfers between devices, body(): lax.psum_scatter(down_grad.astype(jnp.bfloat16), 'ctx', scatter_dimension...  109 us
    reduce_scatter x1, waiting for transfers between devices, body(): lax.psum_scatter(gate_grad.astype(jnp.bfloat16), 'ctx', scatter_dimension...  109 us
    unnamed x2, blocking collectives  88.6 us
    all_gather x1, waiting for transfers between devices, body(): lax.all_gather(gate_master.astype(jnp.bfloat16), 'ctx', axis=1, tiled=True)  83.4 us
  transfers between devices with their start and end apart: 47, of which 30 were waited for; matrix products, arithmetic and copies ran while one was open for 19% of the time, Pallas kernels for 0%

commit v1 on v0

v1 whole, which is shorter than its diff:
```python
from functools import partial

import jax
import jax.numpy as jnp
from jax import lax
from jax.experimental import pallas as pl
from jax.experimental.pallas import tpu as pltpu
from jax.sharding import PartitionSpec as P

D = 1024
HEADS = 16
HEAD_DIM = 64
TOP = 2
BLOCK = 256
STEP = 3
EXP_AXIS = 4

eps_norm = 1e-06
eps_adam = 1e-08
score_scale = 0.125
decay_rate = 0.5
learn_rate = 1.0
weight_decay = 0.1
highest = lax.Precision.HIGHEST
last_dims = (((1,), (1,)), ((), ()))
first_dims = (((0,), (0,)), ((), ()))
bf16 = jnp.bfloat16
f32 = jnp.float32
both = ("ctx", "exp")


def swap_bit(value, bit):
    count = lax.axis_size("ctx") * EXP_AXIS
    return lax.ppermute(value, both, [(d, d ^ (1 << bit)) for d in range(count)])


def flat_index():
    return lax.axis_index("ctx") * EXP_AXIS + lax.axis_index("exp")


def my_bit(bit):
    return (flat_index() >> bit) & 1


def turn(value):
    count = lax.axis_size("ctx") * EXP_AXIS

    def other(d):
        low, high = d & 1, (d >> 2) & 1
        return (d & ~5) | (low << 2) | high

    return lax.ppermute(value, both, [(d, other(d)) for d in range(count)])


def cube_gather(value, bits):
    out = value[None]
    for bit in bits:
        theirs = swap_bit(out, bit)
        low = my_bit(bit) == 0
        out = jnp.concatenate([jnp.where(low, out, theirs), jnp.where(low, theirs, out)], axis=0)
    return out


def cube_scatter(value, bits):
    for bit in bits:
        pairs = value.reshape((value.shape[0] // 2, 2) + value.shape[1:])
        mine = lax.dynamic_index_in_dim(pairs, my_bit(bit), 1, keepdims=False)
        theirs = lax.dynamic_index_in_dim(pairs, 1 - my_bit(bit), 1, keepdims=False)
        got = swap_bit(theirs, bit)
        value = (mine.astype(f32) + got.astype(f32)).astype(value.dtype)
    return value[0]


def pair_groups():
    count = lax.axis_size("ctx")
    return [[c for c in range(low, count, 2)] for low in range(2)]


def gather_expert(shard):
    moved = turn(shard)
    mine = lax.all_gather(moved, "ctx", axis=0, axis_index_groups=pair_groups())
    theirs = swap_bit(mine, 0)
    low = my_bit(0) == 0
    whole = jnp.stack([jnp.where(low, mine, theirs), jnp.where(low, theirs, mine)], axis=1)
    return whole.reshape(-1, shard.shape[1])


def scatter_expert(grad):
    half = lax.axis_size("ctx") // 2
    rows = grad.shape[0] // (2 * half)
    value = grad.reshape(half, 2, rows, grad.shape[1])
    mine = lax.dynamic_index_in_dim(value, my_bit(0), 1, keepdims=False)
    theirs = lax.dynamic_index_in_dim(value, 1 - my_bit(0), 1, keepdims=False)
    got = swap_bit(theirs.astype(bf16), 0)
    total = (mine.astype(f32) + got.astype(f32)).astype(bf16)
    part = lax.psum_scatter(total, "ctx", scatter_dimension=0, axis_index_groups=pair_groups())
    return turn(part)


def lane_mask(width, head, dtype):
    lane = lax.broadcasted_iota(jnp.int32, (1, width), 1)
    return ((lane // HEAD_DIM) == head).astype(dtype)


def fill_bias(ob_ref, head, bias, blocks):
    for d in range(blocks):
        first = (blocks - d - 1) * BLOCK
        window = ob_ref[0, pl.ds(head, 1), pl.ds(first, 2 * BLOCK)]
        wide = jnp.broadcast_to(window, (BLOCK, 2 * BLOCK))
        bias[d] = pltpu.roll(wide, 0, 1, stride=1, stride_axis=0)[:, BLOCK:]


def attend_kernel(blocks, heads, qkv_ref, ob_ref, att_ref, summed_ref, total_ref, bias, km, acc, tot):
    width = qkv_ref.shape[2]
    for head in range(heads):
        mask = lane_mask(width, head, bf16)
        wide_mask = lane_mask(width, head, f32)
        fill_bias(ob_ref, head, bias, blocks)
        km[...] = qkv_ref[1] * mask

        @pl.loop(0, blocks)
        def _(qb):
            rows = pl.ds(pl.multiple_of(qb * BLOCK, BLOCK), BLOCK)
            queries = qkv_ref[0, rows, :] * jnp.asarray(score_scale, bf16)
            acc[...] = jnp.zeros_like(acc)
            tot[...] = jnp.zeros_like(tot)

            @pl.loop(0, qb + 1)
            def _(kb):
                cols = pl.ds(pl.multiple_of(kb * BLOCK, BLOCK), BLOCK)
                score = lax.dot_general(queries, km[cols, :], last_dims, preferred_element_type=f32)
                expo = jnp.exp(score + bias[qb - kb])
                tot[...] += expo[:, :128] + expo[:, 128:]
                acc[...] += jnp.dot(
                    expo.astype(bf16), qkv_ref[2, cols, :], preferred_element_type=f32
                )

            total = jnp.sum(tot[...], axis=1, keepdims=True)
            summed = acc[...]
            if head == 0:
                summed_ref[rows, :] = summed * wide_mask
                total_ref[rows, :] = jnp.broadcast_to(total, summed.shape) * wide_mask
            else:
                summed_ref[rows, :] += summed * wide_mask
                total_ref[rows, :] += jnp.broadcast_to(total, summed.shape) * wide_mask

    @pl.loop(0, blocks)
    def _(qb):
        rows = pl.ds(pl.multiple_of(qb * BLOCK, BLOCK), BLOCK)
        att_ref[rows, :] = (summed_ref[rows, :] / total_ref[rows, :]).astype(bf16)


def attend(qkv, ob):
    _, length, width = qkv.shape
    lanes = min(width, 128)
    heads = lanes // HEAD_DIM
    steps = width // lanes
    blocks = length // BLOCK
    rows = pl.BlockSpec((length, lanes), lambda i: (0, i))
    return pl.pallas_call(
        partial(attend_kernel, blocks, heads),
        grid=(steps,),
        in_specs=[
            pl.BlockSpec((3, length, lanes), lambda i: (0, 0, i)),
            pl.BlockSpec((1, heads, 2 * length), lambda i: (i, 0, 0)),
        ],
        out_specs=[rows, rows, rows],
        out_shape=[
            jax.ShapeDtypeStruct((length, width), bf16),
            jax.ShapeDtypeStruct((length, width), f32),
            jax.ShapeDtypeStruct((length, width), f32),
        ],
        scratch_shapes=[
            pltpu.VMEM((blocks, BLOCK, BLOCK), f32),
            pltpu.VMEM((length, lanes), bf16),
            pltpu.VMEM((BLOCK, lanes), f32),
            pltpu.VMEM((BLOCK, 128), f32),
        ],
        compiler_params=pltpu.CompilerParams(vmem_limit_bytes=48 << 20),
        cost_estimate=pl.CostEstimate(
            flops=4 * length * length * width, bytes_accessed=20 * length * width, transcendentals=0
        ),
        name="attend",
    )(qkv, ob.reshape(steps, heads, 2 * length))


def attend_back_kernel(
    blocks, heads, qkv_ref, ob_ref, da_ref, summed_ref, total_ref, dqkv_ref, diag_ref,
    bias, diff, qm, km, dm, dt, acc_q, acc_k, acc_v,
):
    width = qkv_ref.shape[2]
    acc_q[...] = jnp.zeros_like(acc_q)
    acc_k[...] = jnp.zeros_like(acc_k)
    acc_v[...] = jnp.zeros_like(acc_v)
    for head in range(heads):
        mask = lane_mask(width, head, bf16)
        wide_mask = lane_mask(width, head, f32)
        fill_bias(ob_ref, head, bias, blocks)
        diff[...] = jnp.zeros_like(diff)
        qm[...] = qkv_ref[0] * (mask * jnp.asarray(score_scale, bf16))
        km[...] = qkv_ref[1] * mask

        @pl.loop(0, blocks)
        def _(qb):
            rows = pl.ds(pl.multiple_of(qb * BLOCK, BLOCK), BLOCK)
            grad = da_ref[rows, :].astype(f32)
            total = total_ref[rows, :]
            dm[rows, :] = (grad / total * wide_mask).astype(bf16)
            inner = jnp.sum(grad * summed_ref[rows, :] / (total * total) * wide_mask, axis=1, keepdims=True)
            dt[rows, :] = jnp.broadcast_to(-inner, (BLOCK, 128))

        @pl.loop(0, blocks)
        def _(qb):
            rows = pl.ds(pl.multiple_of(qb * BLOCK, BLOCK), BLOCK)
            queries = qm[rows, :]
            grads = dm[rows, :]
            shift = dt[rows, :][:, :1]

            @pl.loop(0, qb + 1)
            def _(kb):
                cols = pl.ds(pl.multiple_of(kb * BLOCK, BLOCK), BLOCK)
                keys = km[cols, :]
                score = lax.dot_general(queries, keys, last_dims, preferred_element_type=f32)
                expo = jnp.exp(score + bias[qb - kb])
                probs = lax.dot_general(
                    grads, qkv_ref[2, cols, :], last_dims, preferred_element_type=f32
                )
                dscore = (expo * (probs + shift)).astype(bf16)
                diff[qb - kb] += dscore.astype(f32)
                acc_q[rows, :] += jnp.dot(dscore, keys, preferred_element_type=f32)
                acc_k[cols, :] += lax.dot_general(
                    dscore, queries, first_dims, preferred_element_type=f32
                )
                acc_v[cols, :] += lax.dot_general(
                    expo.astype(bf16), grads, first_dims, preferred_element_type=f32
                )

        lower = lax.broadcasted_iota(jnp.int32, (8, 2 * BLOCK), 0)
        for d in range(blocks):

            def add_rows(i, fold):
                part = diff[d, pl.ds(pl.multiple_of(i * 8, 8), 8), :]
                wide = jnp.concatenate([jnp.zeros((8, BLOCK), f32), part], axis=1)
                return fold + pltpu.roll(wide, 2 * BLOCK - 8 * i, 1)

            fold = lax.fori_loop(0, BLOCK // 8, add_rows, jnp.zeros((8, 2 * BLOCK), f32))
            for bit in (1, 2, 4):
                fold = jnp.where((lower & bit) != 0, pltpu.roll(fold, 2 * BLOCK - bit, 1), fold)
            diag_ref[0, pl.ds(head * blocks + d, 1), :] = jnp.sum(fold, axis=0, keepdims=True)
    dqkv_ref[0] = (acc_q[...] * score_scale).astype(bf16)
    dqkv_ref[1] = acc_k[...].astype(bf16)
    dqkv_ref[2] = acc_v[...].astype(bf16)


def attend_back(qkv, ob, grad, summed, total):
    _, length, width = qkv.shape
    lanes = min(width, 128)
    heads = lanes // HEAD_DIM
    steps = width // lanes
    blocks = length // BLOCK
    rows = pl.BlockSpec((length, lanes), lambda i: (0, i))
    wide = pl.BlockSpec((3, length, lanes), lambda i: (0, 0, i))
    dqkv, diag = pl.pallas_call(
        partial(attend_back_kernel, blocks, heads),
        grid=(steps,),
        in_specs=[wide, pl.BlockSpec((1, heads, 2 * length), lambda i: (i, 0, 0)), rows, rows, rows],
        out_specs=[wide, pl.BlockSpec((1, heads * blocks, 2 * BLOCK), lambda i: (i, 0, 0))],
        out_shape=[
            jax.ShapeDtypeStruct((3, length, width), bf16),
            jax.ShapeDtypeStruct((steps, heads * blocks, 2 * BLOCK), f32),
        ],
        scratch_shapes=[
            pltpu.VMEM((blocks, BLOCK, BLOCK), f32),
            pltpu.VMEM((blocks, BLOCK, BLOCK), f32),
            pltpu.VMEM((length, lanes), bf16),
            pltpu.VMEM((length, lanes), bf16),
            pltpu.VMEM((length, lanes), bf16),
            pltpu.VMEM((length, 128), f32),
            pltpu.VMEM((length, lanes), f32),
            pltpu.VMEM((length, lanes), f32),
            pltpu.VMEM((length, lanes), f32),
        ],
        compiler_params=pltpu.CompilerParams(vmem_limit_bytes=56 << 20),
        cost_estimate=pl.CostEstimate(
            flops=10 * length * length * width, bytes_accessed=30 * length * width, transcendentals=0
        ),
        name="attend_back",
    )(qkv, ob.reshape(steps, heads, 2 * length), grad, summed, total)
    return dqkv, diag.reshape(steps * heads, blocks, 2 * BLOCK)


def norm_back(norm_input, factor, gain_wide, grad_normed):
    scaled = grad_normed * gain_wide
    gain_grad = jnp.sum(grad_normed * norm_input * factor, axis=(0, 1))
    mean_term = jnp.mean(scaled * norm_input, axis=-1, keepdims=True)
    return (factor * scaled - norm_input * factor * factor * factor * mean_term, gain_grad)


def adamw_step(master, gradient, first_old, second_old):
    first_new = decay_rate * first_old + (1.0 - decay_rate) * gradient
    second_new = decay_rate * second_old + (1.0 - decay_rate) * gradient * gradient
    correct = 1.0 - decay_rate**STEP
    update = -learn_rate * (
        first_new / correct / (jnp.sqrt(second_new / correct) + eps_adam) + weight_decay * master
    )
    return (gradient, first_new, second_new, update)


def body(tokens, cotangent, bucket_ids, routes, *state):
    masters, firsts, seconds = state[:9], state[9:18], state[18:]
    (
        qkv_master, out_master, router_master, gain_attn_master, gain_mix_master, table_master,
        gate_master, up_master, down_master,
    ) = masters
    micro, tok_rows = tokens.shape[0], tokens.shape[2]
    cycle = lax.axis_size("ctx")
    count = cycle * EXP_AXIS
    all_bits = list(range(count.bit_length() - 1))
    length = tok_rows * cycle
    group = cycle // micro
    width = D // group
    place = lax.axis_index("ctx")
    head_group = place % group
    rows = D // count
    table_rows = table_master.shape[0]
    experts_all = router_master.shape[1]
    capacity = 5 * tok_rows * TOP // (4 * experts_all)

    tok = tokens[:, 0]
    seq = lax.all_to_all(jnp.repeat(tok, group, axis=0), "ctx", 0, 0, tiled=True)
    seq = seq.reshape(length, D)

    cols = qkv_master.astype(bf16).reshape(3, rows, group, width).transpose(2, 0, 1, 3)
    cols = jnp.concatenate([cols] * micro, axis=0)
    cols = lax.all_to_all(cols, "ctx", 0, 0, tiled=True)
    cols = cube_gather(cols, (0, 1))
    w_qkv = cols.transpose(2, 1, 0, 3, 4).reshape(3, D, width)

    small = jnp.concatenate(
        [
            router_master.reshape(-1), gain_attn_master, gain_mix_master, table_master,
        ]
    ).astype(bf16)
    small = cube_gather(small, all_bits)
    edges = (0, rows * experts_all, rows * (experts_all + 1), rows * (experts_all + 2))
    router_bf = small[:, : edges[1]].reshape(D, experts_all)
    gain_attn = small[:, edges[1] : edges[2]].reshape(D).astype(f32)
    gain_mix = small[:, edges[2] : edges[3]].reshape(D).astype(f32)
    table = small[:, edges[3] :].reshape(HEADS, -1)
    bucket_count = table.shape[1]
    router_wide = router_bf.astype(f32)
    bucket_hits = bucket_ids[:, None] == jnp.arange(bucket_count, dtype=jnp.int32)[None, :]
    own_heads = HEADS // group
    own_table = lax.dynamic_slice_in_dim(table, head_group * own_heads, own_heads, 0)
    offset_bias = lax.dot_general(
        own_table, bucket_hits.astype(bf16), last_dims, preferred_element_type=f32
    )
    offset_bias = jnp.pad(offset_bias, ((0, 0), (1, 0)))[:, :-1]

    w_gate = gather_expert(gate_master[0].astype(bf16))
    w_up = gather_expert(up_master[0].astype(bf16))
    w_out = lax.all_gather(out_master.astype(bf16), both, axis=0, tiled=True)
    w_down = gather_expert(down_master[0].astype(bf16))

    seq_wide = seq.astype(f32)
    seq_factor = lax.rsqrt(jnp.mean(seq_wide * seq_wide, axis=-1, keepdims=True) + eps_norm)
    normed = (seq_wide * seq_factor * gain_attn).astype(bf16)
    qkv = jnp.einsum("td,cde->cte", normed, w_qkv, preferred_element_type=f32).astype(bf16)
    attended, summed, total = attend(qkv, offset_bias)

    back = lax.all_to_all(attended.reshape(cycle, tok_rows, width), "ctx", 0, 0, tiled=True)
    attended_bf = back.reshape(micro, group, tok_rows, width).transpose(0, 2, 1, 3)
    attended_bf = attended_bf.reshape(micro, tok_rows, D)
    inputs = tok.astype(f32)
    factor_attn = lax.rsqrt(jnp.mean(inputs * inputs, axis=-1, keepdims=True) + eps_norm)
    branch = jnp.dot(attended_bf, w_out, preferred_element_type=f32)
    hidden_state = inputs + branch
    factor_mix = lax.rsqrt(jnp.mean(hidden_state * hidden_state, axis=-1, keepdims=True) + eps_norm)
    normed_mix = hidden_state * factor_mix * gain_mix
    normed_bf = normed_mix.astype(bf16)
    logits = jnp.einsum("mtd,de->mte", normed_bf, router_bf, preferred_element_type=f32)
    router_probs = jax.nn.softmax(logits, axis=-1)
    route_rows = routes.reshape(micro, tok_rows, TOP)
    expert_ids = jnp.arange(experts_all, dtype=jnp.int32)
    picked = (route_rows[:, :, :, None] == expert_ids).astype(f32)
    chosen = jnp.sum(picked * router_probs[:, :, None, :], axis=-1)
    chosen_sum = jnp.sum(chosen, axis=-1, keepdims=True)
    gate_share = chosen / chosen_sum
    flat_routes = route_rows.reshape(micro, tok_rows * TOP)
    route_hits = (flat_routes[:, :, None] == expert_ids).astype(jnp.int32)
    before = jnp.cumsum(route_hits, axis=1) - route_hits
    slot_index = flat_routes * capacity + jnp.sum(before * route_hits, axis=-1)
    targets = expert_ids[:, None] * capacity + jnp.arange(capacity, dtype=jnp.int32)[None, :]
    dispatch = (slot_index[:, None, None, :] == targets[None, :, :, None]).astype(bf16)
    entries = jnp.repeat(normed_bf, TOP, axis=1)
    sent_rows = jnp.einsum("mect,mtd->emcd", dispatch, entries, preferred_element_type=f32)
    dy_rows = cotangent.reshape(micro, tok_rows, D).astype(f32)
    scaled_dy = (gate_share[:, :, :, None] * dy_rows[:, :, None, :]).astype(bf16)
    scaled_dy = scaled_dy.reshape(micro, tok_rows * TOP, D)
    sent_grads = jnp.einsum("mect,mtd->emcd", dispatch, scaled_dy, preferred_element_type=f32)

    def to_expert(value):
        return turn(lax.all_to_all(value.astype(bf16), "exp", 0, 0, tiled=True))

    def from_expert(value):
        return lax.all_to_all(turn(value), "exp", 0, 0, tiled=True)

    got_rows = to_expert(sent_rows)
    got_grads = to_expert(sent_grads)
    slots = got_rows.shape
    flat_rows = got_rows.reshape(-1, D)
    flat_grads = got_grads.reshape(-1, D)
    gate_pre = jnp.dot(flat_rows, w_gate, preferred_element_type=f32)
    up_pre = jnp.dot(flat_rows, w_up, preferred_element_type=f32)
    gelu_out, gelu_pull = jax.vjp(partial(jax.nn.gelu, approximate=True), gate_pre)
    units = (gelu_out * up_pre).astype(bf16)
    out_rows = jnp.dot(units, w_down, preferred_element_type=f32).astype(bf16)
    back_out = from_expert(out_rows.reshape(slots))
    grad_units = lax.dot_general(flat_grads, w_down, last_dims, preferred_element_type=f32)
    down_grad = lax.dot_general(units, flat_grads, first_dims, preferred_element_type=f32)
    grad_gate = gelu_pull(grad_units * up_pre)[0].astype(bf16)
    grad_up = (grad_units * gelu_out).astype(bf16)
    grad_rows = lax.dot_general(grad_gate, w_gate, last_dims, preferred_element_type=f32)
    grad_rows = grad_rows + lax.dot_general(grad_up, w_up, last_dims, preferred_element_type=f32)
    back_grad = from_expert(grad_rows.astype(bf16).reshape(slots))
    gate_grad = lax.dot_general(flat_rows, grad_gate, first_dims, preferred_element_type=f32)
    up_grad = lax.dot_general(flat_rows, grad_up, first_dims, preferred_element_type=f32)
    expert_sums = [
        scatter_expert(member.astype(bf16))[None].astype(f32)
        for member in (gate_grad, up_grad, down_grad)
    ]

    returned = jnp.einsum("mect,emcd->mtd", dispatch, back_out, preferred_element_type=f32)
    returned = returned.reshape(micro, tok_rows, TOP, D)
    mix_out = jnp.sum(gate_share[:, :, :, None] * returned, axis=2)
    output = (hidden_state + mix_out).astype(bf16)
    grad_entries = jnp.einsum("mect,emcd->mtd", dispatch, back_grad, preferred_element_type=f32)
    grad_entries = grad_entries.reshape(micro, tok_rows, TOP, D)
    grad_gates = jnp.sum(dy_rows[:, :, None, :] * returned, axis=-1)
    grad_chosen = grad_gates / chosen_sum - jnp.sum(grad_gates * chosen, axis=-1, keepdims=True) / (
        chosen_sum * chosen_sum
    )
    grad_probs = jnp.sum(grad_chosen[:, :, :, None] * picked, axis=2)
    grad_logits = router_probs * (
        grad_probs - jnp.sum(router_probs * grad_probs, axis=-1, keepdims=True)
    )
    router_grad = jnp.einsum("mtd,mte->de", normed_bf.astype(f32), grad_logits, precision=highest)
    grad_normed = jnp.sum(grad_entries, axis=2) + jnp.einsum(
        "mte,de->mtd", grad_logits, router_wide, precision=highest
    )
    grad_hidden, gain_mix_grad = norm_back(hidden_state, factor_mix, gain_mix, grad_normed)
    grad_hidden = grad_hidden + dy_rows
    grad_branch = grad_hidden.astype(bf16)
    grad_attended = jnp.einsum("mte,de->mtd", grad_branch, w_out, preferred_element_type=f32)
    grad_attended = grad_attended.astype(bf16).reshape(micro, tok_rows, group, width)
    grad_attended = grad_attended.transpose(0, 2, 1, 3).reshape(cycle, tok_rows, width)
    grad_attended = lax.all_to_all(grad_attended, "ctx", 0, 0, tiled=True).reshape(length, width)
    out_grad = jnp.einsum("mtd,mte->de", attended_bf, grad_branch, preferred_element_type=f32)
    out_sum = cube_scatter(out_grad.astype(bf16).reshape(count, rows, D), all_bits).astype(f32)

    dqkv, diag = attend_back(qkv, offset_bias, grad_attended, summed, total)
    partial_normed = jnp.einsum("cte,cde->td", dqkv, w_qkv, preferred_element_type=f32)
    partial_normed = partial_normed.astype(bf16).reshape(cycle, tok_rows, D)
    pieces = lax.all_to_all(partial_normed, "ctx", 0, 0, tiled=True)
    grad_normed_attn = jnp.sum(pieces.reshape(micro, group, tok_rows, D).astype(f32), axis=1)
    grad_inputs, gain_attn_grad = norm_back(inputs, factor_attn, gain_attn, grad_normed_attn)
    grad_inputs = grad_inputs + grad_hidden

    qkv_grad = jnp.einsum("td,cte->cde", normed, dqkv, preferred_element_type=f32)
    qkv_grad = qkv_grad.astype(bf16).reshape(3, cycle, EXP_AXIS, rows, width)
    qkv_grad = cube_scatter(qkv_grad.transpose(2, 1, 0, 3, 4), (0, 1))
    qkv_grad = lax.all_to_all(qkv_grad, "ctx", 0, 0, tiled=True)
    qkv_sum = jnp.sum(qkv_grad.reshape(micro, group, 3, rows, width).astype(f32), axis=0)
    qkv_sum = qkv_sum.transpose(1, 2, 0, 3).reshape(3, rows, D)

    blocks = length // BLOCK
    offset_grad = jnp.zeros((own_heads, 2 * length), f32)
    for d in range(blocks):
        first = (blocks - d - 1) * BLOCK
        offset_grad = offset_grad + jnp.pad(
            diag[:, d], ((0, 0), (first, 2 * length - first - 2 * BLOCK))
        )
    offset_grad = jnp.pad(offset_grad[:, 1:], ((0, 0), (0, 1)))
    own_grad = jnp.dot(offset_grad, bucket_hits.astype(f32), precision=highest)
    table_grad = lax.dynamic_update_slice_in_dim(
        jnp.zeros((HEADS, bucket_count), f32), own_grad, head_group * own_heads, 0
    )
    small_grads = jnp.concatenate(
        [
            router_grad.reshape(count, -1), gain_attn_grad.reshape(count, -1),
            gain_mix_grad.reshape(count, -1), table_grad.reshape(count, -1),
        ],
        axis=1,
    )
    small_sum = cube_scatter(small_grads, all_bits)
    gradients = (
        qkv_sum,
        out_sum,
        small_sum[: edges[1]].reshape(rows, experts_all),
        small_sum[edges[1] : edges[2]],
        small_sum[edges[2] : edges[3]],
        small_sum[edges[3] :],
        *expert_sums,
    )
    results = [
        adamw_step(master, gradient, first_old, second_old)
        for master, gradient, first_old, second_old in zip(masters, gradients, firsts, seconds)
    ]
    flat = [result[kind] for kind in range(4) for result in results]
    return (output.reshape(tokens.shape), grad_inputs.reshape(tokens.shape), *flat)


def solution(mesh):
    token_spec = P(None, "exp", "ctx", None)
    weight_specs = (
        P(None, both, None), P(both, None), P(both, None), P(both), P(both), P(both),
        P("exp", "ctx", None), P("exp", "ctx", None), P("exp", "ctx", None),
    )
    return jax.shard_map(
        body,
        mesh=mesh,
        in_specs=(token_spec, token_spec, P(), token_spec) + weight_specs * 3,
        out_specs=(token_spec, token_spec) + weight_specs * 4,
        check_vma=False,
    )
```

time: 2230 us -> 757 us (0.34)
  waiting for transfers between devices: 1410 us -> 235 us
  local copies, waits for them, and re-layouts: 307 us -> 61.3 us
  blocking collectives: 127 us -> 0 us
  starting transfers between devices: 32.7 us -> 156 us
  matrix products: 218 us -> 107 us
  Pallas kernels: 0 us -> 86.4 us
    reduce_scatter x4 -> x3, waiting for transfers between devices: 469 us -> 0.02 us  [scatter_expert(): lax.psum_scatter(total, 'ctx', scatter_dimension=0, axis_index_groups=pai...]
    unnamed x15 -> x7, waiting for transfers between devices: 275 us -> 0.18 us
    ppermute x30 -> x35, waiting for transfers between devices: 389 us -> 124 us  [the longest x25 80.2 us: swap_bit(): return lax.ppermute(value, both, [(d, d ^ 1 << bit) for d in range(count)])]
    all_gather x7 -> x4, waiting for transfers between devices: 262 us -> 59.9 us  [the longest x3 59.9 us: gather_expert(): mine = lax.all_gather(moved, 'ctx', axis=0, axis_index_groups=pair_groups())]
    dot_general x62 -> x19, matrix products: 211 us -> 97.1 us  [the longest x1 15.2 us: body(): gate_pre = jnp.dot(flat_rows, w_gate, preferred_element_type=f32)]
    reshape x23 -> x14, local copies, waits for them, and re-layouts: 102 us -> 8.19 us  [the longest x1 3.49 us: body(): grad_entries = grad_entries.reshape(micro, tok_rows, TOP, D)]
    unnamed x2 -> x0, blocking collectives: 88.6 us -> none
    pallas_call x0 -> x2, Pallas kernels: none -> 86.4 us  [the longest x1 67.9 us: attend_back(): pl.pallas_call(partial(attend_back_kernel, blocks, heads), grid=(steps,),...]
  transfers between devices with their start and end apart: 47 -> 52, of which waited for: 30 -> 25; matrix products, arithmetic and copies ran while one was open for 19% -> 26% of each run, Pallas kernels for 0% -> 12%
where the time goes in v1:
time: 757 us; the launch traced here: 748 us
  waiting for transfers between devices  235 us (31%)
  starting transfers between devices  156 us (21%)
  matrix products  107 us (14%)
  other arithmetic  87.4 us (12%)
  Pallas kernels  86.4 us (11%)
  local copies, waits for them, and re-layouts  61.3 us (8%)
  between operations  16 us (2%)
    ppermute x25, waiting for transfers between devices, swap_bit(): return lax.ppermute(value, both, [(d, d ^ 1 << bit) for d in range(count)])  80.2 us
    pallas_call x1, Pallas kernels, attend_back(): pl.pallas_call(partial(attend_back_kernel, blocks, heads), grid=(steps,),...  67.9 us
    all_gather x3, waiting for transfers between devices, gather_expert(): mine = lax.all_gather(moved, 'ctx', axis=0, axis_index_groups=pair_groups())  59.9 us
    ppermute x10, waiting for transfers between devices, turn(): return lax.ppermute(value, both, [(d, other(d)) for d in range(count)])  43.8 us
    ppermute x25, starting transfers between devices, swap_bit(): return lax.ppermute(value, both, [(d, d ^ 1 << bit) for d in range(count)])  40.9 us
    ppermute x10, starting transfers between devices, turn(): return lax.ppermute(value, both, [(d, other(d)) for d in range(count)])  35.6 us
    all_to_all x2, starting transfers between devices, from_expert(): return lax.all_to_all(turn(value), 'exp', 0, 0, tiled=True)  21 us
    all_to_all x2, starting transfers between devices, to_expert(): return turn(lax.all_to_all(value.astype(bf16), 'exp', 0, 0, tiled=True))  19.6 us
  transfers between devices with their start and end apart: 52, of which 25 were waited for; matrix products, arithmetic and copies ran while one was open for 26% of the time, Pallas kernels for 12%

profile of v1, /device:TPU:5, one launch (start us, length us, event | category | flops | bytes accessed | tf_op | source)
XLA Modules:
  0.0 748.5 jit_solution(2088389348824715406)
XLA Ops:
  14.3 9.4 %collective-permute-done.10 = bf16[128,2816]{1,0:T(8,128)(2,1)S(1)} collective-permute-done((bf16[128,2816]{1,0:T(8,128)(2,1)S(1)}, bf16[128,2816]{1,0:T(8,128)(2,1)S(1)}, u32[]{:S(2)}, u32[]{:S(2)}) %collective-permute-start.10) | collective-permute-done | bytes 720928 | tf_op jit(solution)/shard_map/ppermute | solution.py:52
  40.3 7.7 %all-to-all-start.1 = ((bf16[8,128,1024]{2,1,0:T(8,128)(2,1)}), bf16[8,128,1024]{2,1,0:T(8,128)(2,1)S(1)}, u32[]{:S(2)}, u32[]{:S(2)}) async-start(bf16[8,128,1024]{2,1,0:T(8,128)(2,1)} %bitcast.347), calls=%async_computation.1 | async-start | bytes 4194304 | tf_op jit(solution)/shard_map/all_to_all | solution.py:330
  60.2 18.2 %collective-permute-done.4 = bf16[4,208]{1,0:T(4,128)(2,1)S(1)} collective-permute-done((bf16[4,208]{1,0:T(4,128)(2,1)S(1)}, bf16[4,208]{1,0:T(4,128)(2,1)S(1)}, u32[]{:S(2)}, u32[]{:S(2)}) %collective-permute-start.4) | collective-permute-done | bytes 1696 | tf_op jit(solution)/shard_map/ppermute | solution.py:34
  88.6 10.3 %collective-permute-start.6 = (bf16[16,208]{1,0:T(8,128)(2,1)S(1)}, bf16[16,208]{1,0:T(8,128)(2,1)S(1)}, u32[]{:S(2)}, u32[]{:S(2)}) collective-permute-start(bf16[16,208]{1,0:T(8,128)(2,1)S(1)} %pad_maximum_fusion.8), channel_id=1, source_target_pairs={{0,16},{1,17},{2,18},{3,19},{4,20},{5,21},{6,22},{7,23},{8,24},{9,... | collective-permute-start | bytes 19976 | tf_op jit(solution)/shard_map/ppermute | solution.py:34
  102.3 10.2 %collective-permute-done.6 = bf16[16,208]{1,0:T(8,128)(2,1)S(1)} collective-permute-done((bf16[16,208]{1,0:T(8,128)(2,1)S(1)}, bf16[16,208]{1,0:T(8,128)(2,1)S(1)}, u32[]{:S(2)}, u32[]{:S(2)}) %collective-permute-start.6) | collective-permute-done | bytes 6688 | tf_op jit(solution)/shard_map/ppermute | solution.py:34
  127.3 18.5 %attend.1 = (bf16[1024,256]{1,0:T(8,128)(2,1)}, f32[1024,256]{1,0:T(8,128)S(1)}, f32[1024,256]{1,0:T(8,128)S(1)}) custom-call(bf16[3,1024,256]{2,1,0:T(8,128)(2,1)S(1)} %fusion.27.qkv_ref, f32[2,2,2048]{2,1,0:T(2,128)S(1)} %reshape.495.ob_ref), custom_call_target="tpu_custom_call" | custom-call | flops 1073741824 | bytes 5242880 | tf_op jit(solution)/shard_map/attend/pallas_call | solution.py:160
  153.0 14.0 %all-to-all-done.2 = bf16[8,128,256]{2,1,0:T(8,128)(2,1)S(1)} async-done(((bf16[8,128,256]{2,1,0:T(8,128)(2,1)}), bf16[8,128,256]{2,1,0:T(8,128)(2,1)S(1)}, u32[]{:S(2)}, u32[]{:S(2)}) %all-to-all-start.2) | async-done | bytes 524320 | tf_op jit(solution)/shard_map/all_to_all | solution.py:371
  171.9 9.8 %collective-permute-start.11 = (bf16[4,128,2816]{2,1,0:T(8,128)(2,1)}, bf16[4,128,2816]{2,1,0:T(8,128)(2,1)}, u32[]{:S(2)}, u32[]{:S(2)}) collective-permute-start(bf16[4,128,2816]{2,1,0:T(8,128)(2,1)} %bitcast.367), channel_id=1, source_target_pairs={{0,1},{1,0},{2,3},{3,2},{4,5},{5,4},{6,7},{7,6},{8,9},{9,8},{10,11... | collective-permute-start | bytes 8650760 | tf_op jit(solution)/shard_map/ppermute | solution.py:34
  188.3 11.2 %all-to-all-start.5 = ((bf16[4,2,80,1024]{3,2,1,0:T(8,128)(2,1)}), bf16[4,2,80,1024]{3,2,1,0:T(8,128)(2,1)}, u32[]{:S(2)}, u32[]{:S(2)}) async-start(bf16[4,2,80,1024]{3,2,1,0:T(8,128)(2,1)} %copy.403), calls=%async_computation.5 | async-start | bytes 2621440 | tf_op jit(solution)/shard_map/all_to_all | solution.py:403
  199.5 14.3 %all-gather.14.cloned.1.call-done = bf16[1408,1024]{1,0:T(8,128)(2,1)} async-done(((bf16[352,1024]{1,0:T(8,128)(2,1)}), bf16[1408,1024]{1,0:T(8,128)(2,1)}) %all-gather.14.cloned.1.call-update) | async-done | bytes 2883600 | tf_op jit(solution)/shard_map/all_gather | solution.py:81
  222.0 8.4 %all-to-all-start.3 = ((bf16[4,2,80,1024]{3,2,1,0:T(8,128)(2,1)}), bf16[4,2,80,1024]{3,2,1,0:T(8,128)(2,1)}, u32[]{:S(2)}, u32[]{:S(2)}) async-start(bf16[4,2,80,1024]{3,2,1,0:T(8,128)(2,1)} %copy.396), calls=%async_computation.3 | async-start | bytes 2621440 | tf_op jit(solution)/shard_map/all_to_all | solution.py:403
  230.5 45.6 %all-gather.10.cloned.1.call-done = bf16[512,2816]{1,0:T(8,128)(2,1)} async-done(((bf16[128,2816]{1,0:T(8,128)(2,1)}), bf16[512,2816]{1,0:T(8,128)(2,1)}) %all-gather.10.cloned.1.call-update) | async-done | bytes 2883600 | tf_op jit(solution)/shard_map/all_gather | solution.py:81
  296.2 7.8 %fusion.128 = f32[640,2816]{1,0:T(8,128)} fusion(bf16[640,1024]{1,0:T(8,128)(2,1)} %bitcast.50, bf16[2816,1024]{1,0:T(8,128)(2,1)S(1)} %bitcast.353), kind=kOutput, calls=%fused_computation.299 | convolution fusion | flops 3690987520 | bytes 14286848 | tf_op jit(solution)/shard_map/dot_general | solution.py:419
  318.7 15.2 %fusion.7 = (bf16[640,2816]{1,0:T(8,128)(2,1)S(1)}, bf16[640,2816]{1,0:T(8,128)(2,1)}, bf16[640,2816]{1,0:T(8,128)(2,1)}) fusion(f32[640,2816]{1,0:T(8,128)} %fusion.128, f32[640,2816]{1,0:T(8,128)} %fusion.127, bf16[640,1024]{1,0:T(8,128)(2,1)S(1)} %bitcast.401, bf16[1024,2816]{1,0:T(8,128)(2,1)S(1)} %bitcast.359), kind=kOutput, calls=%fused_computation.9 | convolution fusion | flops 3737845760 | bytes 32309248 | tf_op jit(solution)/shard_map/dot_general | solution.py:413
  333.9 13.8 %convolution_convert_fusion.2 = bf16[1024,2816]{1,0:T(8,128)(2,1)S(1)} fusion(bf16[640,1024]{1,0:T(8,128)(2,1)S(1)} %bitcast.402, bf16[640,2816]{1,0:T(8,128)(2,1)S(1)} %get-tuple-element.389), kind=kOutput, calls=%fused_computation.24 | convolution fusion | flops 3693871104 | bytes 10682368 | tf_op jit(solution)/shard_map/dot_general | solution.py:426
  361.7 7.3 convolution_convert_fusion.1
  396.9 7.2 collective-permute-done.16
  404.1 14.6 %all-to-all-start.6 = ((bf16[4,2,80,1024]{3,2,1,0:T(8,128)(2,1)}), bf16[4,2,80,1024]{3,2,1,0:T(8,128)(2,1)}, u32[]{:S(2)}, u32[]{:S(2)}) async-start(bf16[4,2,80,1024]{3,2,1,0:T(8,128)(2,1)} %collective-permute-done.16), calls=%async_computation.6 | async-start | bytes 2621440 | tf_op jit(solution)/shard_map/all_to_all | solution.py:406
  424.9 9.1 %all-to-all-done.6 = bf16[4,2,80,1024]{3,2,1,0:T(8,128)(2,1)} async-done(((bf16[4,2,80,1024]{3,2,1,0:T(8,128)(2,1)}), bf16[4,2,80,1024]{3,2,1,0:T(8,128)(2,1)}, u32[]{:S(2)}, u32[]{:S(2)}) %all-to-all-start.6) | async-done | bytes 1310752 | tf_op jit(solution)/shard_map/all_to_all | solution.py:406
  503.2 67.9 %attend_back.1 = (bf16[3,1024,256]{2,1,0:T(8,128)(2,1)}, f32[2,8,512]{2,1,0:T(8,128)}) custom-call(bf16[3,1024,256]{2,1,0:T(8,128)(2,1)} %copy-done.1, f32[2,2,2048]{2,1,0:T(2,128)} %copy-done, bf16[1024,256]{1,0:T(8,128)(2,1)} %bitcast.56.da_ref, f32[1024,256]{1,0:T(8,128)} %copy-done.2, f32[1024,256]{1,0:T(8,128)} %copy-done.3), custom_call_target="tpu_custom_call" | custom-call | flops 2684354560 | bytes 7864320 | tf_op jit(solution)/shard_map/attend_back/pallas_call | solution.py:263
  598.6 10.9 %collective-permute-done.20 = bf16[8,32,1024]{2,1,0:T(8,128)(2,1)S(1)} collective-permute-done((bf16[8,32,1024]{2,1,0:T(8,128)(2,1)}, bf16[8,32,1024]{2,1,0:T(8,128)(2,1)S(1)}, u32[]{:S(2)}, u32[]{:S(2)}) %collective-permute-start.20) | collective-permute-done | bytes 524320 | tf_op jit(solution)/shard_map/ppermute | solution.py:34
  622.1 18.4 %collective-permute-done.22 = bf16[2,32,1024]{2,1,0:T(8,128)(2,1)S(1)} collective-permute-done((bf16[2,32,1024]{2,1,0:T(8,128)(2,1)S(1)}, bf16[2,32,1024]{2,1,0:T(8,128)(2,1)S(1)}, u32[]{:S(2)}, u32[]{:S(2)}) %collective-permute-start.22) | collective-permute-done | bytes 131104 | tf_op jit(solution)/shard_map/ppermute | solution.py:34
  644.9 18.8 %all-to-all-done.8 = bf16[8,128,1024]{2,1,0:T(8,128)(2,1)} async-done(((bf16[8,128,1024]{2,1,0:T(8,128)(2,1)}), bf16[8,128,1024]{2,1,0:T(8,128)(2,1)}, u32[]{:S(2)}, u32[]{:S(2)}) %all-to-all-start.8) | async-done | bytes 2097184 | tf_op jit(solution)/shard_map/all_to_all | solution.py:464
  663.7 13.7 %all-to-all-start.9 = ((bf16[8,3,32,256]{3,2,1,0:T(8,128)(2,1)}), bf16[8,3,32,256]{3,2,1,0:T(8,128)(2,1)S(1)}, u32[]{:S(2)}, u32[]{:S(2)}) async-start(bf16[8,3,32,256]{3,2,1,0:T(8,128)(2,1)} %fusion.76), calls=%async_computation.9 | async-start | bytes 786432 | tf_op jit(solution)/shard_map/all_to_all | solution.py:472
  (462 shorter events, 350.4 us)
Async XLA Ops:
  7.2 160.6 %all-gather.8.cloned.1.call-start = ((), (), s32[]{:S(2)}) async-start(), calls=%async_computation.13 | async-start | bytes 2162688 | tf_op jit(solution)/shard_map/all_gather | solution.py:362
  8.9 163.1 %all-gather.12.cloned.1.call-start = ((), (), s32[]{:S(2)}) async-start(), calls=%async_computation.18 | async-start | bytes 3604480 | tf_op jit(solution)/shard_map/all_gather | solution.py:81
  33.5 44.9 %collective-permute-start.12 = (bf16[352,1024]{1,0:T(8,128)(2,1)}, bf16[352,1024]{1,0:T(8,128)(2,1)}, u32[]{:S(2)}, u32[]{:S(2)}) collective-permute-start(bf16[352,1024]{1,0:T(8,128)(2,1)} %convert_bitcast_fusion.3), channel_id=1, source_target_pairs={{0,0},{1,4},{2,2},{3,6},{4,1},{5,5},{6,3},{7,7},{8,8},{9,12},{10,1... | collective-permute-start | bytes 2162696 | tf_op jit(solution)/shard_map/ppermute | solution.py:52
  40.3 82.5 %all-to-all-start.1 = ((bf16[8,128,1024]{2,1,0:T(8,128)(2,1)}), bf16[8,128,1024]{2,1,0:T(8,128)(2,1)S(1)}, u32[]{:S(2)}, u32[]{:S(2)}) async-start(bf16[8,128,1024]{2,1,0:T(8,128)(2,1)} %bitcast.347), calls=%async_computation.1 | async-start | bytes 4194304 | tf_op jit(solution)/shard_map/all_to_all | solution.py:330
  48.0 165.7 %all-gather.14.cloned.1.call-start = ((), (), s32[]{:S(2)}) async-start(), calls=%async_computation.19 | async-start | bytes 3604480 | tf_op jit(solution)/shard_map/all_gather | solution.py:81
  50.4 101.8 %collective-permute-start.8 = (bf16[128,2816]{1,0:T(8,128)(2,1)}, bf16[128,2816]{1,0:T(8,128)(2,1)}, u32[]{:S(2)}, u32[]{:S(2)}) collective-permute-start(bf16[128,2816]{1,0:T(8,128)(2,1)} %convert_bitcast_fusion.5), channel_id=1, source_target_pairs={{0,0},{1,4},{2,2},{3,6},{4,1},{5,5},{6,3},{7,7},{8,8},{9,12},{10,1... | collective-permute-start | bytes 2162696 | tf_op jit(solution)/shard_map/ppermute | solution.py:52
  151.7 124.3 %all-gather.10.cloned.1.call-start = ((), (), s32[]{:S(2)}) async-start(), calls=%async_computation.17 | async-start | bytes 3604480 | tf_op jit(solution)/shard_map/all_gather | solution.py:81
  171.9 110.8 %collective-permute-start.11 = (bf16[4,128,2816]{2,1,0:T(8,128)(2,1)}, bf16[4,128,2816]{2,1,0:T(8,128)(2,1)}, u32[]{:S(2)}, u32[]{:S(2)}) collective-permute-start(bf16[4,128,2816]{2,1,0:T(8,128)(2,1)} %bitcast.367), channel_id=1, source_target_pairs={{0,1},{1,0},{2,3},{3,2},{4,5},{5,4},{6,7},{7,6},{8,9},{9,8},{10,11... | collective-permute-start | bytes 8650760 | tf_op jit(solution)/shard_map/ppermute | solution.py:34
  188.3 33.7 %all-to-all-start.5 = ((bf16[4,2,80,1024]{3,2,1,0:T(8,128)(2,1)}), bf16[4,2,80,1024]{3,2,1,0:T(8,128)(2,1)}, u32[]{:S(2)}, u32[]{:S(2)}) async-start(bf16[4,2,80,1024]{3,2,1,0:T(8,128)(2,1)} %copy.403), calls=%async_computation.5 | async-start | bytes 2621440 | tf_op jit(solution)/shard_map/all_to_all | solution.py:403
  213.8 72.1 %collective-permute-start.13 = (bf16[4,352,1024]{2,1,0:T(8,128)(2,1)}, bf16[4,352,1024]{2,1,0:T(8,128)(2,1)}, u32[]{:S(2)}, u32[]{:S(2)}) collective-permute-start(bf16[4,352,1024]{2,1,0:T(8,128)(2,1)} %bitcast.369), channel_id=1, source_target_pairs={{0,1},{1,0},{2,3},{3,2},{4,5},{5,4},{6,7},{7,6},{8,9},{9,8},{10,11... | collective-permute-start | bytes 8650760 | tf_op jit(solution)/shard_map/ppermute | solution.py:34
  222.0 57.9 %all-to-all-start.3 = ((bf16[4,2,80,1024]{3,2,1,0:T(8,128)(2,1)}), bf16[4,2,80,1024]{3,2,1,0:T(8,128)(2,1)}, u32[]{:S(2)}, u32[]{:S(2)}) async-start(bf16[4,2,80,1024]{3,2,1,0:T(8,128)(2,1)} %copy.396), calls=%async_computation.3 | async-start | bytes 2621440 | tf_op jit(solution)/shard_map/all_to_all | solution.py:403
  230.5 468.0 %reduce-scatter.4.cloned.1.call-start = ((), (), s32[]{:S(2)}) async-start(), calls=%async_computation.14 | async-start | bytes 3604480 | tf_op jit(solution)/shard_map/reduce_scatter | solution.py:96
  276.1 39.9 %collective-permute-start.9 = (bf16[4,128,2816]{2,1,0:T(8,128)(2,1)}, bf16[4,128,2816]{2,1,0:T(8,128)(2,1)}, u32[]{:S(2)}, u32[]{:S(2)}) collective-permute-start(bf16[4,128,2816]{2,1,0:T(8,128)(2,1)} %bitcast.371), channel_id=1, source_target_pairs={{0,1},{1,0},{2,3},{3,2},{4,5},{5,4},{6,7},{7,6},{8,9},{9,8},{10,11... | collective-permute-start | bytes 8650760 | tf_op jit(solution)/shard_map/ppermute | solution.py:34
  279.9 30.2 %collective-permute-start.7 = (bf16[4,2,80,1024]{3,2,1,0:T(8,128)(2,1)}, bf16[4,2,80,1024]{3,2,1,0:T(8,128)(2,1)S(1)}, u32[]{:S(2)}, u32[]{:S(2)}) collective-permute-start(bf16[4,2,80,1024]{3,2,1,0:T(8,128)(2,1)} %all-to-all-done.3), channel_id=1, source_target_pairs={{0,0},{1,4},{2,2},{3,6},{4,1},{5,5},{6,3},{7,7},{8,8},{9,12},{10,1... | collective-permute-start | bytes 3932168 | tf_op jit(solution)/shard_map/ppermute | solution.py:52
  373.3 46.7 %collective-permute-start.31 = (bf16[4,128,2816]{2,1,0:T(8,128)(2,1)}, bf16[4,128,2816]{2,1,0:T(8,128)(2,1)}, u32[]{:S(2)}, u32[]{:S(2)}) collective-permute-start(bf16[4,128,2816]{2,1,0:T(8,128)(2,1)} %dynamic-slice_bitcast_fusion.1), channel_id=1, source_target_pairs={{0,1},{1,0},{2,3},{3,2},{4,5},{5,4},{6,7},{7,6},{8,9},{9,8},{10,11... | collective-permute-start | bytes 8650760 | tf_op jit(solution)/shard_map/ppermute | solution.py:34
  392.5 32.3 %collective-permute-start.14 = (bf16[4,2,80,1024]{3,2,1,0:T(8,128)(2,1)}, bf16[4,2,80,1024]{3,2,1,0:T(8,128)(2,1)}, u32[]{:S(2)}, u32[]{:S(2)}) collective-permute-start(bf16[4,2,80,1024]{3,2,1,0:T(8,128)(2,1)} %bitcast.40), channel_id=1, source_target_pairs={{0,0},{1,4},{2,2},{3,6},{4,1},{5,5},{6,3},{7,7},{8,8},{9,12},{10,1... | collective-permute-start | bytes 3932168 | tf_op jit(solution)/shard_map/ppermute | solution.py:52
  404.1 29.9 %all-to-all-start.6 = ((bf16[4,2,80,1024]{3,2,1,0:T(8,128)(2,1)}), bf16[4,2,80,1024]{3,2,1,0:T(8,128)(2,1)}, u32[]{:S(2)}, u32[]{:S(2)}) async-start(bf16[4,2,80,1024]{3,2,1,0:T(8,128)(2,1)} %collective-permute-done.16), calls=%async_computation.6 | async-start | bytes 2621440 | tf_op jit(solution)/shard_map/all_to_all | solution.py:406
  418.7 288.6 %reduce-scatter.6.cloned.1.call-start = ((), (), s32[]{:S(2)}) async-start(), calls=%async_computation.15 | async-start | bytes 3604480 | tf_op jit(solution)/shard_map/reduce_scatter | solution.py:96
  451.0 129.2 %collective-permute-start.33 = (bf16[4,352,1024]{2,1,0:T(8,128)(2,1)}, bf16[4,352,1024]{2,1,0:T(8,128)(2,1)}, u32[]{:S(2)}, u32[]{:S(2)}) collective-permute-start(bf16[4,352,1024]{2,1,0:T(8,128)(2,1)} %dynamic-slice_bitcast_fusion), channel_id=1, source_target_pairs={{0,1},{1,0},{2,3},{3,2},{4,5},{5,4},{6,7},{7,6},{8,9},{9,8},{10,11... | collective-permute-start | bytes 8650760 | tf_op jit(solution)/shard_map/ppermute | solution.py:34
  492.5 101.0 %collective-permute-start.19 = (bf16[16,32,1024]{2,1,0:T(8,128)(2,1)}, bf16[16,32,1024]{2,1,0:T(8,128)(2,1)}, u32[]{:S(2)}, u32[]{:S(2)}) collective-permute-start(bf16[16,32,1024]{2,1,0:T(8,128)(2,1)} %dynamic-slice_bitcast_fusion.3), channel_id=1, source_target_pairs={{0,1},{1,0},{2,3},{3,2},{4,5},{5,4},{6,7},{7,6},{8,9},{9,8},{10,11... | collective-permute-start | bytes 3145736 | tf_op jit(solution)/shard_map/ppermute | solution.py:34
  575.7 88.0 %all-to-all-start.8 = ((bf16[8,128,1024]{2,1,0:T(8,128)(2,1)}), bf16[8,128,1024]{2,1,0:T(8,128)(2,1)}, u32[]{:S(2)}, u32[]{:S(2)}) async-start(bf16[8,128,1024]{2,1,0:T(8,128)(2,1)} %bitcast.373), calls=%async_computation.8 | async-start | bytes 4194304 | tf_op jit(solution)/shard_map/all_to_all | solution.py:464
  580.1 129.1 %reduce-scatter.8.cloned.1.call-start = ((), (), s32[]{:S(2)}) async-start(), calls=%async_computation.16 | async-start | bytes 3604480 | tf_op jit(solution)/shard_map/reduce_scatter | solution.py:96
  612.4 31.7 %collective-permute-start.18 = (bf16[1,8,3,32,256]{4,3,2,1,0:T(8,128)(2,1)S(1)}, bf16[1,8,3,32,256]{4,3,2,1,0:T(8,128)(2,1)S(1)}, u32[]{:S(2)}, u32[]{:S(2)}) collective-permute-start(bf16[1,8,3,32,256]{4,3,2,1,0:T(8,128)(2,1)S(1)} %constant_dynamic-slice_fusion.11), channel_id=1, source_target_pairs={{0,2},{1,3},{2,0},{3,1},{4,6},{5,7},{6,4},{7,5},{8,10},{9,11},{10,... | collective-permute-start | bytes 1179656 | tf_op jit(solution)/shard_map/ppermute | solution.py:34
  641.8 40.9 %collective-permute-start.23 = (bf16[1,32,1024]{2,1,0:T(8,128)(2,1)}, bf16[1,32,1024]{2,1,0:T(8,128)(2,1)}, u32[]{:S(2)}, u32[]{:S(2)}) collective-permute-start(bf16[1,32,1024]{2,1,0:T(8,128)(2,1)} %constant_dynamic-slice_fusion.10), channel_id=1, source_target_pairs={{0,16},{1,17},{2,18},{3,19},{4,20},{5,21},{6,22},{7,23},{8,24},{9,... | collective-permute-start | bytes 196616 | tf_op jit(solution)/shard_map/ppermute | solution.py:34
  (117 other events, 1328.5 us)
Sparse Core Ops, SparseCore 0:
  11.5 65.7 all-gather.7
  79.4 70.5 all-gather.11
  151.6 62.1 all-gather.13
  215.2 60.8 all-gather.9
  361.8 53.9 reduce-scatter.3
  425.0 53.7 reduce-scatter.5
  586.0 88.2 reduce-scatter.7

commit v2 on v1

--- a/solution.py
+++ b/solution.py
@@ -27,6 +27,7 @@
 bf16 = jnp.bfloat16
 f32 = jnp.float32
 both = ("ctx", "exp")
+MESH = pl.DeviceIdType.MESH
 
 
 def swap_bit(value, bit):
@@ -49,7 +50,204 @@
         low, high = d & 1, (d >> 2) & 1
         return (d & ~5) | (low << 2) | high
 
-    return lax.ppermute(value, both, [(d, other(d)) for d in range(count)])
+    got = lax.ppermute(value, both, [(d, other(d)) for d in range(count) if other(d) != d])
+    return jnp.where(my_bit(0) == my_bit(2), value, got)
+
+
+def place_of(flat):
+    return (flat // EXP_AXIS, flat % EXP_AXIS)
+
+
+def greet(partners):
+    barrier = pltpu.get_barrier_semaphore()
+    for partner in partners:
+        pl.semaphore_signal(barrier, inc=1, device_id=place_of(partner), device_id_type=MESH)
+    pl.semaphore_wait(barrier, len(partners))
+
+
+def remote(source, target, send, recv, partner):
+    return pltpu.make_async_remote_copy(
+        src_ref=source, dst_ref=target, send_sem=send, recv_sem=recv,
+        device_id=place_of(partner), device_id_type=MESH,
+    )
+
+
+def exchange_call(kernel, name, number, arrays, shapes, sems):
+    vmem = pl.BlockSpec(memory_space=pltpu.VMEM)
+    sent = sum(array.size * array.dtype.itemsize for array in arrays)
+    return pl.pallas_call(
+        kernel,
+        in_specs=[vmem] * len(arrays),
+        out_specs=[vmem] * len(shapes),
+        out_shape=shapes,
+        scratch_shapes=[pltpu.SemaphoreType.DMA((size,)) for size in sems],
+        compiler_params=pltpu.CompilerParams(
+            collective_id=number, has_side_effects=True, vmem_limit_bytes=48 << 20
+        ),
+        cost_estimate=pl.CostEstimate(flops=0, bytes_accessed=8 * sent, transcendentals=0),
+        name=name,
+    )(*arrays)
+
+
+def opening_kernel(cycle, group, tok_ref, col_ref, seq_ref, all_ref, s1, r1, s2, r2, s3, r3):
+    me = flat_index()
+    ctx, exp = place_of(me)
+    greet([me ^ (rel * EXP_AXIS) for rel in range(1, cycle)] + [me ^ rel for rel in range(1, EXP_AXIS)])
+    copies = []
+    for rel in range(1, cycle):
+        peer = ctx ^ rel
+        copies.append(
+            remote(
+                col_ref.at[lax.rem(peer, group)], all_ref.at[exp, ctx], s1.at[rel], r1.at[rel],
+                me ^ (rel * EXP_AXIS),
+            )
+        )
+        copies[-1].start()
+    tokens = []
+    for rel in range(1, cycle):
+        peer = ctx ^ rel
+        tokens.append(
+            remote(
+                tok_ref.at[peer // group], seq_ref.at[ctx], s2.at[rel], r2.at[rel],
+                me ^ (rel * EXP_AXIS),
+            )
+        )
+        tokens[-1].start()
+    all_ref[exp, ctx] = col_ref[lax.rem(ctx, group)]
+    seq_ref[ctx] = tok_ref[ctx // group]
+    for copy in copies:
+        copy.wait()
+    forwards = []
+    for rel in range(1, EXP_AXIS):
+        forwards.append(
+            remote(all_ref.at[exp], all_ref.at[exp], s3.at[rel], r3.at[rel], me ^ rel)
+        )
+        forwards[-1].start()
+    for copy in tokens + forwards:
+        copy.wait()
+
+
+def opening(tok, cols):
+    cycle = lax.axis_size("ctx")
+    group = cycle // tok.shape[0]
+    return exchange_call(
+        partial(opening_kernel, cycle, group), "opening", 0, [tok, cols],
+        [
+            jax.ShapeDtypeStruct((cycle,) + tok.shape[1:], tok.dtype),
+            jax.ShapeDtypeStruct((EXP_AXIS, cycle) + cols.shape[1:], cols.dtype),
+        ],
+        [cycle, cycle, cycle, cycle, EXP_AXIS, EXP_AXIS],
+    )
+
+
+def cycle_kernel(cycle, in_ref, out_ref, send, recv):
+    me = flat_index()
+    ctx, _ = place_of(me)
+    greet([me ^ (rel * EXP_AXIS) for rel in range(1, cycle)])
+    copies = []
+    for rel in range(1, cycle):
+        copies.append(
+            remote(
+                in_ref.at[ctx ^ rel], out_ref.at[ctx], send.at[rel], recv.at[rel],
+                me ^ (rel * EXP_AXIS),
+            )
+        )
+        copies[-1].start()
+    out_ref[ctx] = in_ref[ctx]
+    for copy in copies:
+        copy.wait()
+
+
+def cycle_swap(value, name, number):
+    cycle = lax.axis_size("ctx")
+    return exchange_call(
+        partial(cycle_kernel, cycle), name, number, [value],
+        [jax.ShapeDtypeStruct(value.shape, value.dtype)], [cycle, cycle],
+    )[0]
+
+
+def closing_kernel(cycle, col_ref, small_ref, out_ref, all_ref, s1, r1, s2, r2):
+    me = flat_index()
+    ctx, _ = place_of(me)
+    count = cycle * EXP_AXIS
+    greet([me ^ rel for rel in range(1, count)])
+    copies = []
+    for rel in range(1, cycle):
+        copies.append(
+            remote(
+                col_ref.at[ctx ^ rel], out_ref.at[ctx], s1.at[rel], r1.at[rel], me ^ (rel * EXP_AXIS)
+            )
+        )
+        copies[-1].start()
+    for rel in range(1, count):
+        copies.append(
+            remote(small_ref.at[me ^ rel], all_ref.at[me], s2.at[rel], r2.at[rel], me ^ rel)
+        )
+        copies[-1].start()
+    out_ref[ctx] = col_ref[ctx]
+    all_ref[me] = small_ref[me]
+    for copy in copies:
+        copy.wait()
+
+
+def closing(cols, small):
+    cycle = lax.axis_size("ctx")
+    count = cycle * EXP_AXIS
+    return exchange_call(
+        partial(closing_kernel, cycle), "closing", 6, [cols, small],
+        [jax.ShapeDtypeStruct(x.shape, x.dtype) for x in (cols, small)],
+        [cycle, cycle, count, count],
+    )
+
+
+def plane_kernel(forward, arrays, *refs):
+    ins, outs, send, recv = refs[:arrays], refs[arrays : 2 * arrays], refs[-2], refs[-1]
+    me = flat_index()
+    ctx, exp = place_of(me)
+    greet([me ^ rel for rel in range(1, 2 * EXP_AXIS)])
+    base = (ctx // 2) * 2
+    ctx_low, exp_low = lax.rem(ctx, 2), lax.rem(exp, 2)
+    for index in range(arrays):
+        for e in range(EXP_AXIS):
+            own = jnp.logical_and(exp == e, ctx_low == exp_low)
+            sem = index * EXP_AXIS
+            if forward:
+                to_ctx, to_exp = base + e % 2, (e // 2) * 2 + ctx_low
+                slot = exp
+            else:
+                to_ctx, to_exp = base + exp_low, e
+                slot = (exp // 2) * 2 + ctx_low
+            copy = remote(
+                ins[index].at[e], outs[index].at[slot], send.at[sem + e], recv.at[sem + slot],
+                to_ctx * EXP_AXIS + to_exp,
+            )
+
+            @pl.when(jnp.logical_not(own))
+            def _():
+                copy.start()
+
+            @pl.when(own)
+            def _():
+                outs[index][e] = ins[index][e]
+
+    for index in range(arrays):
+        for e in range(EXP_AXIS):
+            own = jnp.logical_and(exp == e, ctx_low == exp_low)
+            sem = index * EXP_AXIS + e
+            done = remote(ins[index].at[e], outs[index].at[e], send.at[sem], recv.at[sem], me ^ 1)
+
+            @pl.when(jnp.logical_not(own))
+            def _():
+                done.wait()
+
+
+def plane_swap(values, forward, name, number):
+    count = len(values)
+    return exchange_call(
+        partial(plane_kernel, forward, count), name, number, list(values),
+        [jax.ShapeDtypeStruct(x.shape, x.dtype) for x in values],
+        [count * EXP_AXIS, count * EXP_AXIS],
+    )
 
 
 def cube_gather(value, bits):
@@ -58,6 +256,16 @@
         theirs = swap_bit(out, bit)
         low = my_bit(bit) == 0
         out = jnp.concatenate([jnp.where(low, out, theirs), jnp.where(low, theirs, out)], axis=0)
+    return out
+
+
+def cube_gather_high(value, bits):
+    out = value[None]
+    for bit in reversed(bits):
+        theirs = swap_bit(out, bit)
+        low = my_bit(bit) == 0
+        out = jnp.stack([jnp.where(low, out, theirs), jnp.where(low, theirs, out)], axis=1)
+        out = out.reshape((-1,) + value.shape)
     return out
 
 
@@ -327,21 +535,21 @@
     capacity = 5 * tok_rows * TOP // (4 * experts_all)
 
     tok = tokens[:, 0]
-    seq = lax.all_to_all(jnp.repeat(tok, group, axis=0), "ctx", 0, 0, tiled=True)
-    seq = seq.reshape(length, D)
-
-    cols = qkv_master.astype(bf16).reshape(3, rows, group, width).transpose(2, 0, 1, 3)
-    cols = jnp.concatenate([cols] * micro, axis=0)
-    cols = lax.all_to_all(cols, "ctx", 0, 0, tiled=True)
-    cols = cube_gather(cols, (0, 1))
-    w_qkv = cols.transpose(2, 1, 0, 3, 4).reshape(3, D, width)
-
+    cols = qkv_master.astype(bf16).reshape(3 * rows, group, width).transpose(1, 0, 2)
     small = jnp.concatenate(
         [
             router_master.reshape(-1), gain_attn_master, gain_mix_master, table_master,
         ]
     ).astype(bf16)
-    small = cube_gather(small, all_bits)
+    small_size = small.shape[0]
+    small = jnp.pad(small, (0, 16 * width - small_size)).reshape(1, 16, width)
+    cols = jnp.concatenate([cols, jnp.broadcast_to(small, (group, 16, width))], axis=1)
+    seq, gathered = opening(tok, cols)
+    seq = seq.reshape(length, D)
+    w_qkv = gathered[:, :, : 3 * rows].reshape(EXP_AXIS, cycle, 3, rows, width)
+    w_qkv = w_qkv.transpose(2, 1, 0, 3, 4).reshape(3, D, width)
+    small = gathered[:, :, 3 * rows :].reshape(EXP_AXIS, cycle, 16 * width)[:, :, :small_size]
+    small = small.transpose(1, 0, 2).reshape(count, small_size)
     edges = (0, rows * experts_all, rows * (experts_all + 1), rows * (experts_all + 2))
     router_bf = small[:, : edges[1]].reshape(D, experts_all)
     gain_attn = small[:, edges[1] : edges[2]].reshape(D).astype(f32)
@@ -359,7 +567,7 @@
 
     w_gate = gather_expert(gate_master[0].astype(bf16))
     w_up = gather_expert(up_master[0].astype(bf16))
-    w_out = lax.all_gather(out_master.astype(bf16), both, axis=0, tiled=True)
+    w_out = cube_gather_high(out_master.astype(bf16), all_bits).reshape(D, D)
     w_down = gather_expert(down_master[0].astype(bf16))
 
     seq_wide = seq.astype(f32)
@@ -368,7 +576,7 @@
     qkv = jnp.einsum("td,cde->cte", normed, w_qkv, preferred_element_type=f32).astype(bf16)
     attended, summed, total = attend(qkv, offset_bias)
 
-    back = lax.all_to_all(attended.reshape(cycle, tok_rows, width), "ctx", 0, 0, tiled=True)
+    back = cycle_swap(attended.reshape(cycle, tok_rows, width), "attended_swap", 1)
     attended_bf = back.reshape(micro, group, tok_rows, width).transpose(0, 2, 1, 3)
     attended_bf = attended_bf.reshape(micro, tok_rows, D)
     inputs = tok.astype(f32)
@@ -399,14 +607,9 @@
     scaled_dy = scaled_dy.reshape(micro, tok_rows * TOP, D)
     sent_grads = jnp.einsum("mect,mtd->emcd", dispatch, scaled_dy, preferred_element_type=f32)
 
-    def to_expert(value):
-        return turn(lax.all_to_all(value.astype(bf16), "exp", 0, 0, tiled=True))
-
-    def from_expert(value):
-        return lax.all_to_all(turn(value), "exp", 0, 0, tiled=True)
-
-    got_rows = to_expert(sent_rows)
-    got_grads = to_expert(sent_grads)
+    got_rows, got_grads = plane_swap(
+        (sent_rows.astype(bf16), sent_grads.astype(bf16)), True, "dispatch_swap", 2
+    )
     slots = got_rows.shape
     flat_rows = got_rows.reshape(-1, D)
     flat_grads = got_grads.reshape(-1, D)
@@ -415,14 +618,15 @@
     gelu_out, gelu_pull = jax.vjp(partial(jax.nn.gelu, approximate=True), gate_pre)
     units = (gelu_out * up_pre).astype(bf16)
     out_rows = jnp.dot(units, w_down, preferred_element_type=f32).astype(bf16)
-    back_out = from_expert(out_rows.reshape(slots))
     grad_units = lax.dot_general(flat_grads, w_down, last_dims, preferred_element_type=f32)
     down_grad = lax.dot_general(units, flat_grads, first_dims, preferred_element_type=f32)
     grad_gate = gelu_pull(grad_units * up_pre)[0].astype(bf16)
     grad_up = (grad_units * gelu_out).astype(bf16)
     grad_rows = lax.dot_general(grad_gate, w_gate, last_dims, preferred_element_type=f32)
     grad_rows = grad_rows + lax.dot_general(grad_up, w_up, last_dims, preferred_element_type=f32)
-    back_grad = from_expert(grad_rows.astype(bf16).reshape(slots))
+    back_out, back_grad = plane_swap(
+        (out_rows.reshape(slots), grad_rows.astype(bf16).reshape(slots)), False, "return_swap", 3
+    )
     gate_grad = lax.dot_general(flat_rows, grad_gate, first_dims, preferred_element_type=f32)
     up_grad = lax.dot_general(flat_rows, grad_up, first_dims, preferred_element_type=f32)
     expert_sums = [
@@ -454,14 +658,14 @@
     grad_attended = jnp.einsum("mte,de->mtd", grad_branch, w_out, preferred_element_type=f32)
     grad_attended = grad_attended.astype(bf16).reshape(micro, tok_rows, group, width)
     grad_attended = grad_attended.transpose(0, 2, 1, 3).reshape(cycle, tok_rows, width)
-    grad_attended = lax.all_to_all(grad_attended, "ctx", 0, 0, tiled=True).reshape(length, width)
+    grad_attended = cycle_swap(grad_attended, "grad_swap", 4).reshape(length, width)
     out_grad = jnp.einsum("mtd,mte->de", attended_bf, grad_branch, preferred_element_type=f32)
     out_sum = cube_scatter(out_grad.astype(bf16).reshape(count, rows, D), all_bits).astype(f32)
 
     dqkv, diag = attend_back(qkv, offset_bias, grad_attended, summed, total)
     partial_normed = jnp.einsum("cte,cde->td", dqkv, w_qkv, preferred_element_type=f32)
     partial_normed = partial_normed.astype(bf16).reshape(cycle, tok_rows, D)
-    pieces = lax.all_to_all(partial_normed, "ctx", 0, 0, tiled=True)
+    pieces = cycle_swap(partial_normed, "normed_swap", 5)
     grad_normed_attn = jnp.sum(pieces.reshape(micro, group, tok_rows, D).astype(f32), axis=1)
     grad_inputs, gain_attn_grad = norm_back(inputs, factor_attn, gain_attn, grad_normed_attn)
     grad_inputs = grad_inputs + grad_hidden
@@ -469,9 +673,6 @@
     qkv_grad = jnp.einsum("td,cte->cde", normed, dqkv, preferred_element_type=f32)
     qkv_grad = qkv_grad.astype(bf16).reshape(3, cycle, EXP_AXIS, rows, width)
     qkv_grad = cube_scatter(qkv_grad.transpose(2, 1, 0, 3, 4), (0, 1))
-    qkv_grad = lax.all_to_all(qkv_grad, "ctx", 0, 0, tiled=True)
-    qkv_sum = jnp.sum(qkv_grad.reshape(micro, group, 3, rows, width).astype(f32), axis=0)
-    qkv_sum = qkv_sum.transpose(1, 2, 0, 3).reshape(3, rows, D)
 
     blocks = length // BLOCK
     offset_grad = jnp.zeros((own_heads, 2 * length), f32)
@@ -492,7 +693,11 @@
         ],
         axis=1,
     )
-    small_sum = cube_scatter(small_grads, all_bits)
+    small_grads = jnp.pad(small_grads, ((0, 0), (0, -small_grads.shape[1] % 128)))
+    qkv_grad, small_parts = closing(qkv_grad, small_grads[:, None])
+    qkv_sum = jnp.sum(qkv_grad.reshape(micro, group, 3, rows, width).astype(f32), axis=0)
+    qkv_sum = qkv_sum.transpose(1, 2, 0, 3).reshape(3, rows, D)
+    small_sum = jnp.sum(small_parts[:, 0], axis=0)[:small_size]
     gradients = (
         qkv_sum,
         out_sum,

time: 757 us -> 747 us (0.987)
  Pallas kernels: 86.4 us -> 369 us
  waiting for transfers between devices: 235 us -> 63.3 us
  starting transfers between devices: 156 us -> 47.2 us
  matrix products: 107 us -> 90.1 us
    pallas_call x0 -> x7, Pallas kernels: none -> 283 us  [exchange_call(): pl.pallas_call(kernel, in_specs=[vmem] * len(arrays), out_specs=[vmem] *...]
    all_to_all x10 -> x0, starting transfers between devices: 79.2 us -> none  [the longest x2 21 us: from_expert(): return lax.all_to_all(turn(value), 'exp', 0, 0, tiled=True)]
    all_gather x3, waiting for transfers between devices: 59.9 us -> 0.02 us  [gather_expert(): mine = lax.all_gather(moved, 'ctx', axis=0, axis_index_groups=pair_groups())]
    all_to_all x10 -> x0, waiting for transfers between devices: 50.4 us -> none  [the longest x1 18.8 us: body(): pieces = lax.all_to_all(partial_normed, 'ctx', 0, 0, tiled=True)]
    ppermute x25 -> x18, waiting for transfers between devices: 80.2 us -> 43.8 us  [swap_bit(): return lax.ppermute(value, both, [(d, d ^ 1 << bit) for d in range(count)])]
    ppermute x10 -> x6, waiting for transfers between devices: 43.8 us -> 19.4 us  [turn(): lax.ppermute(value, both, [(d, other(d)) for d in range(count) if other(d...]
    ppermute x25 -> x18, starting transfers between devices: 40.9 us -> 25.7 us  [swap_bit(): return lax.ppermute(value, both, [(d, d ^ 1 << bit) for d in range(count)])]
    ppermute x10 -> x6, starting transfers between devices: 35.6 us -> 21 us  [turn(): lax.ppermute(value, both, [(d, other(d)) for d in range(count) if other(d...]
  transfers between devices with their start and end apart: 52 -> 30, of which waited for: 25 -> 11; matrix products, arithmetic and copies ran while one was open for 26% -> 26% of each run, Pallas kernels for 12% -> 50%
where the time goes in v2:
time: 747 us; the launch traced here: 739 us
  Pallas kernels  369 us (49%)
  other arithmetic  93.9 us (13%)
  matrix products  90.1 us (12%)
  waiting for transfers between devices  63.3 us (8%)
  local copies, waits for them, and re-layouts  59.4 us (8%)
  starting transfers between devices  47.2 us (6%)
  between operations  16.1 us (2%)
    pallas_call x7, Pallas kernels, exchange_call(): pl.pallas_call(kernel, in_specs=[vmem] * len(arrays), out_specs=[vmem] *...  283 us
    pallas_call x1, Pallas kernels, attend_back(): pl.pallas_call(partial(attend_back_kernel, blocks, heads), grid=(steps,),...  67.9 us
    ppermute x18, waiting for transfers between devices, swap_bit(): return lax.ppermute(value, both, [(d, d ^ 1 << bit) for d in range(count)])  43.8 us
    ppermute x18, starting transfers between devices, swap_bit(): return lax.ppermute(value, both, [(d, d ^ 1 << bit) for d in range(count)])  25.7 us
    ppermute x6, starting transfers between devices, turn(): lax.ppermute(value, both, [(d, other(d)) for d in range(count) if other(d...  21 us
    ppermute x6, waiting for transfers between devices, turn(): lax.ppermute(value, both, [(d, other(d)) for d in range(count) if other(d...  19.4 us
    pallas_call x1, Pallas kernels, attend(): pl.pallas_call(partial(attend_kernel, blocks, heads), grid=(steps,), in_s...  18 us
    mul x8, other arithmetic, adamw_step(): -learn_rate  16.3 us
  transfers between devices with their start and end apart: 30, of which 11 were waited for; matrix products, arithmetic and copies ran while one was open for 26% of the time, Pallas kernels for 50%

profile of v2, /device:TPU:5, one launch (start us, length us, event | category | flops | bytes accessed | tf_op | source)
XLA Modules:
  0.0 738.8 jit_solution(8848618029797901303)
XLA Ops:
  13.5 9.3 %collective-permute-done.7 = bf16[128,2816]{1,0:T(8,128)(2,1)} collective-permute-done((bf16[128,2816]{1,0:T(8,128)(2,1)}, bf16[128,2816]{1,0:T(8,128)(2,1)}, u32[]{:S(2)}, u32[]{:S(2)}) %collective-permute-start.7) | collective-permute-done | bytes 720928 | tf_op jit(solution)/shard_map/ppermute | solution.py:53
  31.8 6.4 collective-permute-done.9
  44.1 83.6 %opening.1 = (bf16[8,128,1024]{2,1,0:T(8,128)(2,1)S(1)}, bf16[4,8,112,256]{3,2,1,0:T(8,128)(2,1)S(1)}) custom-call(bf16[2,128,1024]{2,1,0:T(8,128)(2,1)S(1)} %bitcast.352, bf16[4,112,256]{2,1,0:T(8,128)(2,1)S(1)} %pad_maximum_fusion.8.col_ref), custom_call_target="tpu_custom_call" | custom-call | bytes 6029312 | tf_op jit(solution)/shard_map/opening/pallas_call | solution.py:78
  138.3 13.5 %collective-permute-start.1 = (bf16[2,32,1024]{2,1,0:T(8,128)(2,1)S(1)}, bf16[2,32,1024]{2,1,0:T(8,128)(2,1)S(1)}, u32[]{:S(2)}, u32[]{:S(2)}) collective-permute-start(bf16[2,32,1024]{2,1,0:T(8,128)(2,1)S(1)} %maximum_bitcast_fusion), channel_id=1, source_target_pairs={{0,8},{1,9},{2,10},{3,11},{4,12},{5,13},{6,14},{7,15},{8,0},{9,1},... | collective-permute-start | bytes 393224 | tf_op jit(solution)/shard_map/ppermute | solution.py:35
  152.9 14.5 %collective-permute-done.1 = bf16[2,32,1024]{2,1,0:T(8,128)(2,1)S(1)} collective-permute-done((bf16[2,32,1024]{2,1,0:T(8,128)(2,1)S(1)}, bf16[2,32,1024]{2,1,0:T(8,128)(2,1)S(1)}, u32[]{:S(2)}, u32[]{:S(2)}) %collective-permute-start.1) | collective-permute-done | bytes 131104 | tf_op jit(solution)/shard_map/ppermute | solution.py:35
  177.7 9.4 %collective-permute-done.3 = bf16[8,32,1024]{2,1,0:T(8,128)(2,1)} collective-permute-done((bf16[8,32,1024]{2,1,0:T(8,128)(2,1)S(1)}, bf16[8,32,1024]{2,1,0:T(8,128)(2,1)}, u32[]{:S(2)}, u32[]{:S(2)}) %collective-permute-start.3) | collective-permute-done | bytes 524320 | tf_op jit(solution)/shard_map/ppermute | solution.py:35
  193.5 18.0 %attend.1 = (bf16[1024,256]{1,0:T(8,128)(2,1)S(1)}, f32[1024,256]{1,0:T(8,128)S(1)}, f32[1024,256]{1,0:T(8,128)S(1)}) custom-call(bf16[3,1024,256]{2,1,0:T(8,128)(2,1)S(1)} %copy-done.9, f32[2,2,2048]{2,1,0:T(2,128)S(1)} %reshape.449.ob_ref), custom_call_target="tpu_custom_call" | custom-call | flops 1073741824 | bytes 5242880 | tf_op jit(solution)/shard_map/attend/pallas_call | solution.py:368
  212.5 22.4 %attended_swap.1 = bf16[8,128,256]{2,1,0:T(8,128)(2,1)S(1)} custom-call(bf16[8,128,256]{2,1,0:T(8,128)(2,1)S(1)} %bitcast.359), custom_call_target="tpu_custom_call" | custom-call | bytes 4194304 | tf_op jit(solution)/shard_map/attended_swap/pallas_call | solution.py:78
  259.3 32.1 %dispatch_swap.1 = (bf16[4,2,80,1024]{3,2,1,0:T(8,128)(2,1)S(1)}, bf16[4,2,80,1024]{3,2,1,0:T(8,128)(2,1)S(1)}) custom-call(bf16[4,2,80,1024]{3,2,1,0:T(8,128)(2,1)S(1)} %fusion.36.refs_0_, bf16[4,2,80,1024]{3,2,1,0:T(8,128)(2,1)S(1)} %fusion.37.refs_1_), custom_call_target="tpu_custom_call" | custom-call | bytes 20971520 | tf_op jit(solution)/shard_map/dispatch_swap/pallas_call | solution.py:78
  305.7 9.1 %fusion.115 = f32[640,2816]{1,0:T(8,128)} fusion(bf16[640,1024]{1,0:T(8,128)(2,1)S(1)} %bitcast.361, bf16[2816,1024]{1,0:T(8,128)(2,1)} %bitcast.378), kind=kOutput, calls=%fused_computation.267 | convolution fusion | flops 3690987520 | bytes 14286848 | tf_op jit(solution)/shard_map/dot_general | solution.py:621
  314.8 5.9 fusion.114
  323.4 15.1 %fusion.7 = (bf16[640,2816]{1,0:T(8,128)(2,1)S(1)}, bf16[640,2816]{1,0:T(8,128)(2,1)}, bf16[640,2816]{1,0:T(8,128)(2,1)}) fusion(f32[640,2816]{1,0:T(8,128)} %fusion.115, f32[640,2816]{1,0:T(8,128)} %fusion.114, bf16[640,1024]{1,0:T(8,128)(2,1)S(1)} %bitcast.364, bf16[1024,2816]{1,0:T(8,128)(2,1)S(1)} %bitcast.382), kind=kOutput, calls=%fused_computation.9 | convolution fusion | flops 3737845760 | bytes 32309248 | tf_op jit(solution)/shard_map/dot_general | solution.py:616
  361.2 7.3 convolution_convert_fusion.1
  374.7 6.2 convolution_convert_fusion.4
  380.9 5.9 add_convert_fusion
  386.9 32.3 %return_swap.1 = (bf16[4,2,80,1024]{3,2,1,0:T(8,128)(2,1)S(1)}, bf16[4,2,80,1024]{3,2,1,0:T(8,128)(2,1)S(1)}) custom-call(bf16[4,2,80,1024]{3,2,1,0:T(8,128)(2,1)S(1)} %bitcast.356, bf16[4,2,80,1024]{3,2,1,0:T(8,128)(2,1)S(1)} %bitcast.357), custom_call_target="tpu_custom_call" | custom-call | bytes 20971520 | tf_op jit(solution)/shard_map/return_swap/pallas_call | solution.py:78
  435.4 7.4 %convolution_convert_fusion = bf16[2816,1024]{1,0:T(8,128)(2,1)S(1)} fusion(bf16[640,2816]{1,0:T(8,128)(2,1)} %get-tuple-element.410, bf16[640,1024]{1,0:T(8,128)(2,1)S(1)} %bitcast.362), kind=kOutput, calls=%fused_computation.22 | convolution fusion | flops 3693871104 | bytes 10682368 | tf_op jit(solution)/shard_map/dot_general | solution.py:622
  461.5 28.7 %grad_swap.1 = bf16[8,128,256]{2,1,0:T(8,128)(2,1)S(1)} custom-call(bf16[8,128,256]{2,1,0:T(8,128)(2,1)S(1)} %bitcast.354), custom_call_target="tpu_custom_call" | custom-call | bytes 4194304 | tf_op jit(solution)/shard_map/grad_swap/pallas_call | solution.py:78
  491.0 67.9 %attend_back.1 = (bf16[3,1024,256]{2,1,0:T(8,128)(2,1)}, f32[2,8,512]{2,1,0:T(8,128)}) custom-call(bf16[3,1024,256]{2,1,0:T(8,128)(2,1)} %fusion.23.qkv_ref, f32[2,2,2048]{2,1,0:T(2,128)} %copy-done.2, bf16[1024,256]{1,0:T(8,128)(2,1)} %bitcast.358, f32[1024,256]{1,0:T(8,128)} %copy-done.10, f32[1024,256]{1,0:T(8,128)} %copy-done.11), custom_call_target="tpu_custom_call" | custom-call | flops 2684354560 | bytes 7864320 | tf_op jit(solution)/shard_map/attend_back/pallas_call | solution.py:471
  562.2 44.4 %normed_swap.1 = bf16[8,128,1024]{2,1,0:T(8,128)(2,1)S(1)} custom-call(bf16[8,128,1024]{2,1,0:T(8,128)(2,1)S(1)} %bitcast.353), custom_call_target="tpu_custom_call" | custom-call | bytes 16777216 | tf_op jit(solution)/shard_map/normed_swap/pallas_call | solution.py:78
  620.7 5.7 fusion.8
  640.6 6.2 collective-permute-done.12
  647.0 39.3 %closing.1 = (bf16[8,3,32,256]{3,2,1,0:T(8,128)(2,1)S(1)}, f32[32,1,256]{2,1,0:T(1,128)S(1)}) custom-call(bf16[8,3,32,256]{3,2,1,0:T(8,128)(2,1)S(1)} %fusion.64.col_ref, f32[32,1,256]{2,1,0:T(1,128)S(1)} %broadcast_in_dim.17.small_ref), custom_call_target="tpu_custom_call" | custom-call | bytes 3407872 | tf_op jit(solution)/shard_map/closing/pallas_call | solution.py:78
  712.7 5.2 add_multiply_fusion.2
  (453 shorter events, 226.6 us)
Async XLA Ops:
  7.2 236.3 %all-gather.9.cloned.1.call-start = ((), (), s32[]{:S(2)}) async-start(), calls=%async_computation.7 | async-start | bytes 3604480 | tf_op jit(solution)/shard_map/all_gather | solution.py:289
  9.7 13.1 %collective-permute-start.7 = (bf16[128,2816]{1,0:T(8,128)(2,1)}, bf16[128,2816]{1,0:T(8,128)(2,1)}, u32[]{:S(2)}, u32[]{:S(2)}) collective-permute-start(bf16[128,2816]{1,0:T(8,128)(2,1)} %convert_bitcast_fusion.4), channel_id=1, source_target_pairs={{1,4},{3,6},{4,1},{6,3},{9,12},{11,14},{12,9},{14,11},{17,20},{19,... | collective-permute-start | bytes 2162696 | tf_op jit(solution)/shard_map/ppermute | solution.py:53
  24.9 228.3 %all-gather.11.cloned.1.call-start = ((), (), s32[]{:S(2)}) async-start(), calls=%async_computation.8 | async-start | bytes 3604480 | tf_op jit(solution)/shard_map/all_gather | solution.py:289
  25.0 13.1 %collective-permute-start.9 = (bf16[352,1024]{1,0:T(8,128)(2,1)S(1)}, bf16[352,1024]{1,0:T(8,128)(2,1)S(1)}, u32[]{:S(2)}, u32[]{:S(2)}) collective-permute-start(bf16[352,1024]{1,0:T(8,128)(2,1)S(1)} %convert_bitcast_fusion.3), channel_id=1, source_target_pairs={{1,4},{3,6},{4,1},{6,3},{9,12},{11,14},{12,9},{14,11},{17,20},{19,... | collective-permute-start | bytes 2162696 | tf_op jit(solution)/shard_map/ppermute | solution.py:53
  29.5 108.0 %collective-permute-start = (bf16[1,32,1024]{2,1,0:T(8,128)(2,1)}, bf16[1,32,1024]{2,1,0:T(8,128)(2,1)}, u32[]{:S(2)}, u32[]{:S(2)}) collective-permute-start(bf16[1,32,1024]{2,1,0:T(8,128)(2,1)} %convert_bitcast_fusion.6), channel_id=1, source_target_pairs={{0,16},{1,17},{2,18},{3,19},{4,20},{5,21},{6,22},{7,23},{8,24},{9,... | collective-permute-start | bytes 196616 | tf_op jit(solution)/shard_map/ppermute | solution.py:35
  39.2 254.3 %all-gather.7.cloned.1.call-start = ((), (), s32[]{:S(2)}) async-start(), calls=%async_computation.6 | async-start | bytes 3604480 | tf_op jit(solution)/shard_map/all_gather | solution.py:289
  40.2 135.1 %collective-permute-start.5 = (bf16[128,2816]{1,0:T(8,128)(2,1)}, bf16[128,2816]{1,0:T(8,128)(2,1)}, u32[]{:S(2)}, u32[]{:S(2)}) collective-permute-start(bf16[128,2816]{1,0:T(8,128)(2,1)} %convert_bitcast_fusion.5), channel_id=1, source_target_pairs={{1,4},{3,6},{4,1},{6,3},{9,12},{11,14},{12,9},{14,11},{17,20},{19,... | collective-permute-start | bytes 2162696 | tf_op jit(solution)/shard_map/ppermute | solution.py:53
  138.3 29.1 %collective-permute-start.1 = (bf16[2,32,1024]{2,1,0:T(8,128)(2,1)S(1)}, bf16[2,32,1024]{2,1,0:T(8,128)(2,1)S(1)}, u32[]{:S(2)}, u32[]{:S(2)}) collective-permute-start(bf16[2,32,1024]{2,1,0:T(8,128)(2,1)S(1)} %maximum_bitcast_fusion), channel_id=1, source_target_pairs={{0,8},{1,9},{2,10},{3,11},{4,12},{5,13},{6,14},{7,15},{8,0},{9,1},... | collective-permute-start | bytes 393224 | tf_op jit(solution)/shard_map/ppermute | solution.py:35
  175.0 12.2 %collective-permute-start.3 = (bf16[8,32,1024]{2,1,0:T(8,128)(2,1)S(1)}, bf16[8,32,1024]{2,1,0:T(8,128)(2,1)}, u32[]{:S(2)}, u32[]{:S(2)}) collective-permute-start(bf16[8,32,1024]{2,1,0:T(8,128)(2,1)S(1)} %bitcast.403), channel_id=1, source_target_pairs={{0,2},{1,3},{2,0},{3,1},{4,6},{5,7},{6,4},{7,5},{8,10},{9,11},{10,... | collective-permute-start | bytes 1572872 | tf_op jit(solution)/shard_map/ppermute | solution.py:35
  177.5 519.2 %reduce-scatter.4.cloned.1.call-start = ((), (), s32[]{:S(2)}) async-start(), calls=%async_computation.3 | async-start | bytes 3604480 | tf_op jit(solution)/shard_map/reduce_scatter | solution.py:304
  189.5 54.9 %collective-permute-start.4 = (bf16[16,32,1024]{2,1,0:T(8,128)(2,1)}, bf16[16,32,1024]{2,1,0:T(8,128)(2,1)}, u32[]{:S(2)}, u32[]{:S(2)}) collective-permute-start(bf16[16,32,1024]{2,1,0:T(8,128)(2,1)} %bitcast.26), channel_id=1, source_target_pairs={{0,1},{1,0},{2,3},{3,2},{4,5},{5,4},{6,7},{7,6},{8,9},{9,8},{10,11... | collective-permute-start | bytes 3145736 | tf_op jit(solution)/shard_map/ppermute | solution.py:35
  243.6 50.0 %collective-permute-start.8 = (bf16[4,128,2816]{2,1,0:T(8,128)(2,1)}, bf16[4,128,2816]{2,1,0:T(8,128)(2,1)}, u32[]{:S(2)}, u32[]{:S(2)}) collective-permute-start(bf16[4,128,2816]{2,1,0:T(8,128)(2,1)} %bitcast.397), channel_id=1, source_target_pairs={{0,1},{1,0},{2,3},{3,2},{4,5},{5,4},{6,7},{7,6},{8,9},{9,8},{10,11... | collective-permute-start | bytes 8650760 | tf_op jit(solution)/shard_map/ppermute | solution.py:35
  253.1 44.4 %collective-permute-start.10 = (bf16[4,352,1024]{2,1,0:T(8,128)(2,1)}, bf16[4,352,1024]{2,1,0:T(8,128)(2,1)}, u32[]{:S(2)}, u32[]{:S(2)}) collective-permute-start(bf16[4,352,1024]{2,1,0:T(8,128)(2,1)} %bitcast.399), channel_id=1, source_target_pairs={{0,1},{1,0},{2,3},{3,2},{4,5},{5,4},{6,7},{7,6},{8,9},{9,8},{10,11... | collective-permute-start | bytes 8650760 | tf_op jit(solution)/shard_map/ppermute | solution.py:35
  293.5 27.2 %collective-permute-start.6 = (bf16[4,128,2816]{2,1,0:T(8,128)(2,1)}, bf16[4,128,2816]{2,1,0:T(8,128)(2,1)}, u32[]{:S(2)}, u32[]{:S(2)}) collective-permute-start(bf16[4,128,2816]{2,1,0:T(8,128)(2,1)} %bitcast.401), channel_id=1, source_target_pairs={{0,1},{1,0},{2,3},{3,2},{4,5},{5,4},{6,7},{7,6},{8,9},{9,8},{10,11... | collective-permute-start | bytes 8650760 | tf_op jit(solution)/shard_map/ppermute | solution.py:35
  357.8 348.1 %reduce-scatter.6.cloned.1.call-start = ((), (), s32[]{:S(2)}) async-start(), calls=%async_computation.4 | async-start | bytes 3604480 | tf_op jit(solution)/shard_map/reduce_scatter | solution.py:304
  370.4 51.0 %collective-permute-start.20 = (bf16[4,128,2816]{2,1,0:T(8,128)(2,1)}, bf16[4,128,2816]{2,1,0:T(8,128)(2,1)}, u32[]{:S(2)}, u32[]{:S(2)}) collective-permute-start(bf16[4,128,2816]{2,1,0:T(8,128)(2,1)} %dynamic-slice_bitcast_fusion.1), channel_id=1, source_target_pairs={{0,1},{1,0},{2,3},{3,2},{4,5},{5,4},{6,7},{7,6},{8,9},{9,8},{10,11... | collective-permute-start | bytes 8650760 | tf_op jit(solution)/shard_map/ppermute | solution.py:35
  425.5 285.0 %reduce-scatter.8.cloned.1.call-start = ((), (), s32[]{:S(2)}) async-start(), calls=%async_computation.5 | async-start | bytes 3604480 | tf_op jit(solution)/shard_map/reduce_scatter | solution.py:304
  446.2 174.5 %collective-permute-start.22 = (bf16[4,352,1024]{2,1,0:T(8,128)(2,1)}, bf16[4,352,1024]{2,1,0:T(8,128)(2,1)}, u32[]{:S(2)}, u32[]{:S(2)}) collective-permute-start(bf16[4,352,1024]{2,1,0:T(8,128)(2,1)} %dynamic-slice_bitcast_fusion), channel_id=1, source_target_pairs={{0,1},{1,0},{2,3},{3,2},{4,5},{5,4},{6,7},{7,6},{8,9},{9,8},{10,11... | collective-permute-start | bytes 8650760 | tf_op jit(solution)/shard_map/ppermute | solution.py:35
  614.7 20.2 %collective-permute-start.11 = (bf16[2,8,3,32,256]{4,3,2,1,0:T(8,128)(2,1)}, bf16[2,8,3,32,256]{4,3,2,1,0:T(8,128)(2,1)}, u32[]{:S(2)}, u32[]{:S(2)}) collective-permute-start(bf16[2,8,3,32,256]{4,3,2,1,0:T(8,128)(2,1)} %dynamic-slice_bitcast_fusion.4), channel_id=1, source_target_pairs={{0,1},{1,0},{2,3},{3,2},{4,5},{5,4},{6,7},{7,6},{8,9},{9,8},{10,11... | collective-permute-start | bytes 2359304 | tf_op jit(solution)/shard_map/ppermute | solution.py:35
  620.7 16.0 %collective-permute-start.13 = (bf16[16,32,1024]{2,1,0:T(8,128)(2,1)}, bf16[16,32,1024]{2,1,0:T(8,128)(2,1)}, u32[]{:S(2)}, u32[]{:S(2)}) collective-permute-start(bf16[16,32,1024]{2,1,0:T(8,128)(2,1)} %dynamic-slice_bitcast_fusion.3), channel_id=1, source_target_pairs={{0,1},{1,0},{2,3},{3,2},{4,5},{5,4},{6,7},{7,6},{8,9},{9,8},{10,11... | collective-permute-start | bytes 3145736 | tf_op jit(solution)/shard_map/ppermute | solution.py:35
  639.3 48.1 %collective-permute-start.14 = (bf16[8,32,1024]{2,1,0:T(8,128)(2,1)}, bf16[8,32,1024]{2,1,0:T(8,128)(2,1)S(1)}, u32[]{:S(2)}, u32[]{:S(2)}) collective-permute-start(bf16[8,32,1024]{2,1,0:T(8,128)(2,1)} %dynamic-slice_bitcast_fusion.5), channel_id=1, source_target_pairs={{0,2},{1,3},{2,0},{3,1},{4,6},{5,7},{6,4},{7,5},{8,10},{9,11},{10,... | collective-permute-start | bytes 1572872 | tf_op jit(solution)/shard_map/ppermute | solution.py:35
  696.7 15.9 %collective-permute-start.19 = (bf16[128,2816]{1,0:T(8,128)(2,1)}, bf16[128,2816]{1,0:T(8,128)(2,1)}, u32[]{:S(2)}, u32[]{:S(2)}) collective-permute-start(bf16[128,2816]{1,0:T(8,128)(2,1)} %bitcast.416), channel_id=1, source_target_pairs={{1,4},{3,6},{4,1},{6,3},{9,12},{11,14},{12,9},{14,11},{17,20},{19,... | collective-permute-start | bytes 2162696 | tf_op jit(solution)/shard_map/ppermute | solution.py:53
  705.9 13.7 %collective-permute-start.21 = (bf16[128,2816]{1,0:T(8,128)(2,1)}, bf16[128,2816]{1,0:T(8,128)(2,1)S(1)}, u32[]{:S(2)}, u32[]{:S(2)}) collective-permute-start(bf16[128,2816]{1,0:T(8,128)(2,1)} %bitcast.417), channel_id=1, source_target_pairs={{1,4},{3,6},{4,1},{6,3},{9,12},{11,14},{12,9},{14,11},{17,20},{19,... | collective-permute-start | bytes 2162696 | tf_op jit(solution)/shard_map/ppermute | solution.py:53
  710.5 16.9 %collective-permute-start.23 = (bf16[352,1024]{1,0:T(8,128)(2,1)}, bf16[352,1024]{1,0:T(8,128)(2,1)S(1)}, u32[]{:S(2)}, u32[]{:S(2)}) collective-permute-start(bf16[352,1024]{1,0:T(8,128)(2,1)} %bitcast.418), channel_id=1, source_target_pairs={{1,4},{3,6},{4,1},{6,3},{9,12},{11,14},{12,9},{14,11},{17,20},{19,... | collective-permute-start | bytes 2162696 | tf_op jit(solution)/shard_map/ppermute | solution.py:53
  (114 other events, 1159.1 us)
Sparse Core Ops, SparseCore 0:
  25.0 104.9 all-gather.8
  132.1 59.2 all-gather.10
  193.5 70.4 all-gather.6
  358.0 60.4 reduce-scatter.3
  425.6 68.6 reduce-scatter.5
  626.5 70.0 reduce-scatter.7
